TPU v7x, 32 devices: a whole 2x2x4 slice. The times are simulated.
32 devices in a mesh: section: 2 (over core), dp: 4 (over z), mp: 4 (over y, x).
Axes of the slice: x: 2, y: 2, z: 4, core: 2. Of those that a mesh axis runs over, the one named last changes fastest.
Arguments:
- images: bfloat16 [12, 320, 1152], P('dp', 'mp'), may hold values from -6 to 6
- cotangent: bfloat16 [12, 320, 1152], P('dp', 'mp'), may hold values from -6 to 6
- lengths: int32 [12], P('dp'), may hold values from 192 to 320, as said below
- timesteps: int32 [12], P('dp'), may hold values from 0 to 999
- time_table: bfloat16 [1000, 1152], replicated, may hold values from -6 to 6
- norms: float32 [2, 4, 1152], P('section'), may hold values from 0.5 to 1.5
- qkv_weight: bfloat16 [2, 1152, 3, 1152], P('section', None, None, 'mp'), may hold values from -0.1875 to 0.1875
- time_weight: bfloat16 [2, 1152, 2, 1152], P('section', None, None, 'mp'), may hold values from -0.1875 to 0.1875
- out_weight: bfloat16 [2, 1152, 1152], P('section', 'mp'), may hold values from -0.75 to 0.75
- out_bias: float32 [2, 1152], P('section'), may hold values from -3 to 3
- mlp_in_weight: bfloat16 [2, 1152, 4608], P('section', None, 'mp'), may hold values from -0.1875 to 0.1875
- mlp_in_bias: float32 [2, 4608], P('section', 'mp'), may hold values from -3 to 3
- mlp_out_weight: bfloat16 [2, 4608, 1152], P('section', 'mp'), may hold values from -0.09375 to 0.09375
- mlp_out_bias: float32 [2, 1152], P('section'), may hold values from -3 to 3
- rel_bias: float32 [2, 16, 639], P('section', 'mp'), may hold values from -5 to 5
Outputs:
- boundary: float32 [2, 12, 320, 1152], P('section', 'dp', 'mp')
- grad_norms: float32 [2, 4, 1152], P('section')
- grad_qkv: float32 [2, 1152, 3, 1152], P('section', 'dp', None, 'mp')
- grad_time: float32 [2, 1152, 2, 1152], P('section', 'dp', None, 'mp')
- grad_out_weight: float32 [2, 1152, 1152], P('section', 'mp', 'dp')
- grad_out_bias: float32 [2, 1152], P('section')
- grad_mlp_in_weight: float32 [2, 1152, 4608], P('section', 'dp', 'mp')
- grad_mlp_in_bias: float32 [2, 4608], P('section', 'mp')
- grad_mlp_out_weight: float32 [2, 4608, 1152], P('section', 'mp', 'dp')
- grad_mlp_out_bias: float32 [2, 1152], P('section')
- grad_rel_bias: float32 [2, 16, 639], P('section', 'mp')
Inputs may be any that keep to these rules, and one draw needn't show every extreme that they name: `lengths`: some image has exactly 320 tokens.
All inputs are finite; a program needn't handle non-finite values.
Results may differ from a plain program's by a relative error of at most 0.014.
The roundings to bfloat16 on the way count: a program that leaves them out, or rounds other values in their place, can miss the bound.
Values may be sent and summed in bfloat16 or wider, within the bound.
A program may use at most 192 MiB of HBM per device.

v0:
```python
import math

import jax
import jax.numpy as jnp
from jax import lax
from jax.sharding import PartitionSpec as P

EPSILON = 1e-06
NEG_FILL = -1000000000.0


def from_behind(array, axis, by):
    size = lax.axis_size(axis)
    pairs = [(i, i + by) for i in range(size) if 0 <= i + by < size]
    return lax.ppermute(array, axis, pairs)


def layer_norm(values, norm_gain, offset):
    centred = values - jnp.mean(values, axis=-1, keepdims=True)
    spread = jnp.mean(centred * centred, axis=-1, keepdims=True)
    return centred * lax.rsqrt(spread + EPSILON) * norm_gain + offset


def toeplitz(table):
    head_count, offset_count = table.shape
    seq_len = (offset_count + 1) // 2
    flipped = jnp.flip(table, axis=1)
    extended = jnp.concatenate([flipped, jnp.zeros((head_count, 1), jnp.float32)], axis=1)
    repeated = jnp.broadcast_to(extended[:, None, :], (head_count, seq_len, 2 * seq_len))
    repeated = repeated.reshape(head_count, 2 * seq_len * seq_len)
    skewed = repeated[:, seq_len - 1 : seq_len - 1 + seq_len * offset_count]
    return skewed.reshape(head_count, seq_len, offset_count)[:, :, :seq_len]


def widen_rows(rows_low):
    return lax.all_gather(rows_low, "mp", axis=0, tiled=True)


def narrow_rows(left, weight):
    return lax.psum_scatter(
        jnp.dot(left, weight, preferred_element_type=jnp.float32),
        "mp",
        scatter_dimension=0,
        tiled=True,
    )


def grad_widen_rows(rows_low):
    return lax.all_gather(rows_low, "mp", axis=0, tiled=True)


def grad_narrow_rows(left, weight):
    return lax.psum_scatter(
        lax.dot_general(left, weight, (((1,), (1,)), ((), ())), preferred_element_type=jnp.float32),
        "mp",
        scatter_dimension=0,
        tiled=True,
    )


def attention_scores(queries, key_rows, bias_full, key_mask):
    score_scale = 1.0 / math.sqrt(queries.shape[2])
    raw_scores = (
        jnp.einsum("qhd,khd->hqk", queries, key_rows, preferred_element_type=jnp.float32)
        * score_scale
        + bias_full
    )
    return jnp.where(key_mask[None, None, :], raw_scores, NEG_FILL)


def layer_forward(tokens, length, time_token, layer_params):
    (
        norm_rows,
        qkv_flat,
        time_flat,
        out_weight,
        out_bias,
        mlp_in_weight,
        mlp_in_bias,
        mlp_out_weight,
        mlp_out_bias,
        bias_full,
    ) = layer_params
    normed, norm_pull = jax.vjp(layer_norm, tokens, norm_rows[0], norm_rows[1])
    normed_full = widen_rows(normed.astype(jnp.bfloat16))
    seq_len = normed_full.shape[0]
    local_width = qkv_flat.shape[1] // 3
    head_count = bias_full.shape[0]
    head_size = local_width // head_count
    linear = jnp.dot(normed_full, qkv_flat, preferred_element_type=jnp.float32)
    time_part = jnp.dot(time_token[None, :], time_flat, preferred_element_type=jnp.float32)
    queries = (linear[:, :local_width] + time_part[:, :local_width]).astype(jnp.bfloat16)
    key_rows = linear[:, local_width : 2 * local_width].astype(jnp.bfloat16)
    values = (linear[:, 2 * local_width :] + time_part[:, local_width:]).astype(jnp.bfloat16)
    queries = queries.reshape(seq_len, head_count, head_size)
    key_rows = key_rows.reshape(seq_len, head_count, head_size)
    values = values.reshape(seq_len, head_count, head_size)
    key_mask = jnp.arange(seq_len, dtype=jnp.int32) < length
    scores = attention_scores(queries, key_rows, bias_full, key_mask)
    row_peak = jnp.max(scores, axis=-1, keepdims=True)
    log_total = row_peak + jnp.log(jnp.sum(jnp.exp(scores - row_peak), axis=-1, keepdims=True))
    probability = jnp.exp(scores - log_total)
    attended = jnp.einsum(
        "hqk,khd->qhd", probability.astype(jnp.bfloat16), values, preferred_element_type=jnp.float32
    )
    attended = attended.reshape(seq_len, local_width).astype(jnp.bfloat16)
    mixed_rows = tokens + narrow_rows(attended, out_weight) + out_bias
    normed_two, norm_pull_two = jax.vjp(layer_norm, mixed_rows, norm_rows[2], norm_rows[3])
    normed_two_full = widen_rows(normed_two.astype(jnp.bfloat16))
    hidden = (
        jnp.dot(normed_two_full, mlp_in_weight, preferred_element_type=jnp.float32) + mlp_in_bias
    )
    activated = jax.nn.gelu(hidden).astype(jnp.bfloat16)
    output = mixed_rows + narrow_rows(activated, mlp_out_weight) + mlp_out_bias
    kept = (
        norm_pull,
        normed_full,
        queries,
        key_rows,
        values,
        probability,
        attended,
        norm_pull_two,
        normed_two_full,
        hidden,
        activated,
    )
    return (output, kept)


def layer_backward(tokens, length, time_token, layer_params, grad_out):
    (
        norm_rows,
        qkv_flat,
        time_flat,
        out_weight,
        out_bias,
        mlp_in_weight,
        mlp_in_bias,
        mlp_out_weight,
        mlp_out_bias,
        bias_full,
    ) = layer_params
    _, kept = layer_forward(tokens, length, time_token, layer_params)
    (
        norm_pull,
        normed_full,
        queries,
        key_rows,
        values,
        probability,
        attended,
        norm_pull_two,
        normed_two_full,
        hidden,
        activated,
    ) = kept
    seq_len = normed_full.shape[0]
    local_width = qkv_flat.shape[1] // 3
    head_count = bias_full.shape[0]
    head_size = local_width // head_count
    score_scale = 1.0 / math.sqrt(head_size)
    contract_rows = (((0,), (0,)), ((), ()))
    contract_cols = (((1,), (1,)), ((), ()))
    grad_branch_two = grad_out.astype(jnp.bfloat16)
    mlp_out_bias_grad = jnp.sum(grad_branch_two.astype(jnp.float32), axis=0)
    grad_two_full = grad_widen_rows(grad_branch_two)
    mlp_out_grad = lax.dot_general(
        activated, grad_two_full, contract_rows, preferred_element_type=jnp.float32
    )
    grad_activated = lax.dot_general(
        grad_two_full, mlp_out_weight, contract_cols, preferred_element_type=jnp.float32
    )
    _, gelu_pull = jax.vjp(jax.nn.gelu, hidden)
    grad_hidden = gelu_pull(grad_activated)[0].astype(jnp.bfloat16)
    mlp_in_bias_grad = jnp.sum(grad_hidden.astype(jnp.float32), axis=0)
    mlp_in_grad = lax.dot_general(
        normed_two_full, grad_hidden, contract_rows, preferred_element_type=jnp.float32
    )
    grad_normed_two = grad_narrow_rows(grad_hidden, mlp_in_weight)
    grad_mixed_part, gain_two_grad, offset_two_grad = norm_pull_two(grad_normed_two)
    grad_mixed = grad_out + grad_mixed_part
    grad_branch = grad_mixed.astype(jnp.bfloat16)
    out_bias_grad = jnp.sum(grad_branch.astype(jnp.float32), axis=0)
    grad_branch_full = grad_widen_rows(grad_branch)
    out_grad = lax.dot_general(
        attended, grad_branch_full, contract_rows, preferred_element_type=jnp.float32
    )
    grad_attended = lax.dot_general(
        grad_branch_full, out_weight, contract_cols, preferred_element_type=jnp.float32
    )
    grad_attended = grad_attended.astype(jnp.bfloat16).reshape(seq_len, head_count, head_size)
    grad_probability = jnp.einsum(
        "qhd,khd->hqk", grad_attended, values, preferred_element_type=jnp.float32
    )
    grad_values = jnp.einsum(
        "hqk,qhd->khd",
        probability.astype(jnp.bfloat16),
        grad_attended,
        preferred_element_type=jnp.float32,
    )
    row_inner = jnp.sum(probability * grad_probability, axis=-1, keepdims=True)
    grad_scores = (probability * (grad_probability - row_inner)).astype(jnp.bfloat16)
    grad_queries = (
        jnp.einsum("hqk,khd->qhd", grad_scores, key_rows, preferred_element_type=jnp.float32)
        * score_scale
    )
    grad_keys = (
        jnp.einsum("hqk,qhd->khd", grad_scores, queries, preferred_element_type=jnp.float32)
        * score_scale
    )
    grad_project = jnp.concatenate(
        [
            grad_queries.reshape(seq_len, local_width),
            grad_keys.reshape(seq_len, local_width),
            grad_values.reshape(seq_len, local_width),
        ],
        axis=1,
    ).astype(jnp.bfloat16)
    qkv_grad = lax.dot_general(
        normed_full, grad_project, contract_rows, preferred_element_type=jnp.float32
    )
    column_sums = jnp.sum(grad_project.astype(jnp.float32), axis=0)
    time_columns = jnp.concatenate([column_sums[:local_width], column_sums[2 * local_width :]])
    time_grad = time_token.astype(jnp.float32)[:, None] * time_columns[None, :]
    grad_normed = grad_narrow_rows(grad_project, qkv_flat)
    grad_tokens_part, gain_grad, offset_grad = norm_pull(grad_normed)
    grad_tokens = grad_mixed + grad_tokens_part
    norms_grad = jnp.stack([gain_grad, offset_grad, gain_two_grad, offset_two_grad])
    gradients = (
        norms_grad,
        qkv_grad,
        time_grad,
        out_grad,
        out_bias_grad,
        mlp_in_grad,
        mlp_in_bias_grad,
        mlp_out_grad,
        mlp_out_bias_grad,
        grad_scores.astype(jnp.float32),
    )
    return (grad_tokens, gradients)


def write_slot(store, slot_index, value, active):
    previous = lax.dynamic_index_in_dim(store, slot_index, 0, keepdims=False)
    return lax.dynamic_update_index_in_dim(store, jnp.where(active, value, previous), slot_index, 0)


def weight_members(totals, model_width, local_width):
    return (
        totals[1].reshape(model_width, 3, local_width),
        totals[2].reshape(model_width, 2, local_width),
        totals[3],
        totals[5],
        totals[7],
    )


def local(
    images,
    cotangent,
    lengths,
    timesteps,
    time_table,
    norms,
    qkv_weight,
    time_weight,
    out_weight,
    out_bias,
    mlp_in_weight,
    mlp_in_bias,
    mlp_out_weight,
    mlp_out_bias,
    rel_bias,
):
    model_rank = lax.axis_index("mp")
    section_rank = lax.axis_index("section")
    micro_total = images.shape[0]
    row_count = images.shape[1]
    model_width = images.shape[2]
    local_width = qkv_weight.shape[3]
    qkv_flat = qkv_weight[0].reshape(model_width, 3 * local_width)
    time_flat = time_weight[0].reshape(model_width, 2 * local_width)
    bias_full, bias_pull = jax.vjp(toeplitz, rel_bias[0])
    layer_params = (
        norms[0],
        qkv_flat,
        time_flat,
        out_weight[0],
        out_bias[0],
        mlp_in_weight[0],
        mlp_in_bias[0],
        mlp_out_weight[0],
        mlp_out_bias[0],
        bias_full,
    )
    row_index = model_rank * row_count + jnp.arange(row_count, dtype=jnp.int32)

    def image_inputs(slot_index):
        length = lax.dynamic_index_in_dim(lengths, slot_index, 0, keepdims=False)
        step_index = lax.dynamic_index_in_dim(timesteps, slot_index, 0, keepdims=False)
        time_token = lax.dynamic_index_in_dim(time_table, step_index, 0, keepdims=False)
        row_mask = (row_index < length).astype(jnp.float32)[:, None]
        return (length, time_token, row_mask)

    kept_inputs = jnp.zeros((micro_total, row_count, model_width), jnp.bfloat16)
    boundary = jnp.zeros((micro_total, row_count, model_width), jnp.float32)
    received = jnp.zeros((row_count, model_width), jnp.bfloat16)
    for tick_index in range(micro_total + 1):
        micro_index = tick_index - section_rank
        active = (micro_index >= 0) & (micro_index < micro_total)
        slot_index = jnp.clip(micro_index, 0, micro_total - 1)
        length, time_token, row_mask = image_inputs(slot_index)
        arriving = jnp.where(section_rank == 0, images[min(tick_index, micro_total - 1)], received)
        output, _ = layer_forward(arriving.astype(jnp.float32), length, time_token, layer_params)
        kept_inputs = write_slot(kept_inputs, slot_index, arriving, active)
        boundary = write_slot(boundary, slot_index, output * row_mask, active & (section_rank == 1))
        if tick_index < micro_total:
            received = from_behind(output.astype(jnp.bfloat16), "section", 1)
    totals = None
    incoming = jnp.zeros((row_count, model_width), jnp.bfloat16)
    for tick_index in range(micro_total + 1):
        micro_index = micro_total - tick_index - section_rank
        active = (micro_index >= 0) & (micro_index < micro_total)
        slot_index = jnp.clip(micro_index, 0, micro_total - 1)
        length, time_token, row_mask = image_inputs(slot_index)
        given_grad = cotangent[max(micro_total - 1 - tick_index, 0)].astype(jnp.float32) * row_mask
        grad_out = jnp.where(section_rank == 1, given_grad, incoming.astype(jnp.float32))
        grad_out = jnp.where(active, grad_out, 0.0)
        tokens = lax.dynamic_index_in_dim(kept_inputs, slot_index, 0, keepdims=False).astype(
            jnp.float32
        )
        grad_tokens, gradients = layer_backward(tokens, length, time_token, layer_params, grad_out)
        if totals is None:
            totals = gradients
        else:
            totals = jax.tree.map(jnp.add, totals, gradients)
        boundary = write_slot(boundary, slot_index, grad_tokens, active & (section_rank == 0))
        if tick_index < micro_total:
            incoming = from_behind(grad_tokens.astype(jnp.bfloat16), "section", -1)
    final_qkv, final_time, final_out, final_mlp_in, final_mlp_out = weight_members(
        totals, model_width, local_width
    )
    summed = (
        lax.psum_scatter(
            final_qkv.astype(jnp.bfloat16), "dp", scatter_dimension=0, tiled=True
        ).astype(jnp.float32),
        lax.psum_scatter(
            final_time.astype(jnp.bfloat16), "dp", scatter_dimension=0, tiled=True
        ).astype(jnp.float32),
        lax.psum_scatter(
            final_out.astype(jnp.bfloat16), "dp", scatter_dimension=1, tiled=True
        ).astype(jnp.float32),
        lax.psum_scatter(
            final_mlp_in.astype(jnp.bfloat16), "dp", scatter_dimension=0, tiled=True
        ).astype(jnp.float32),
        lax.psum_scatter(
            final_mlp_out.astype(jnp.bfloat16), "dp", scatter_dimension=1, tiled=True
        ).astype(jnp.float32),
    )
    rel_grad = bias_pull(totals[9])[0]
    table_sum = lax.psum((rel_grad, totals[6]), "dp")
    shared = lax.psum((totals[0], totals[4], totals[8]), ("dp", "mp"))
    return (
        boundary[None],
        shared[0][None],
        summed[0][None],
        summed[1][None],
        summed[2][None],
        shared[1][None],
        summed[3][None],
        table_sum[1][None],
        summed[4][None],
        shared[2][None],
        table_sum[0][None],
    )


def solution(mesh):
    in_specs = (
        P("dp", "mp", None),
        P("dp", "mp", None),
        P("dp"),
        P("dp"),
        P(),
        P("section", None, None),
        P("section", None, None, "mp"),
        P("section", None, None, "mp"),
        P("section", "mp", None),
        P("section", None),
        P("section", None, "mp"),
        P("section", "mp"),
        P("section", "mp", None),
        P("section", None),
        P("section", "mp", None),
    )
    out_specs = (
        P("section", "dp", "mp", None),
        P("section", None, None),
        P("section", "dp", None, "mp"),
        P("section", "dp", None, "mp"),
        P("section", "mp", "dp"),
        P("section", None),
        P("section", "dp", "mp"),
        P("section", "mp"),
        P("section", "mp", "dp"),
        P("section", None),
        P("section", "mp", None),
    )
    return jax.shard_map(local, mesh=mesh, in_specs=in_specs, out_specs=out_specs, check_vma=False)
```

profile of v0, /device:TPU:0, one launch (start us, length us, event | category | flops | bytes accessed | tf_op | source)
XLA Modules:
  0.0 1424.4 jit_solution(13536548415185787617)
XLA Ops:
  11.6 12.5 all_gather.72
  41.3 3.0 slice.263
  44.3 7.8 reshape.780
  52.2 3.0 slice.264
  65.1 30.3 %reduce-scatter.75.cloned.1.call-done = f32[80,1152]{1,0:T(8,128)} async-done(((f32[320,1152]{1,0:T(8,128)}), f32[80,1152]{1,0:T(8,128)}) %reduce-scatter.75.cloned.1.call-update) | async-done | bytes 368656
  97.0 11.7 all_gather.73
  108.7 5.4 fusion.17
  119.8 25.0 %reduce-scatter.77.cloned.1.call-done = f32[80,1152]{1,0:T(8,128)} async-done(((f32[320,1152]{1,0:T(8,128)}), f32[80,1152]{1,0:T(8,128)}) %reduce-scatter.77.cloned.1.call-update) | async-done | bytes 368656
  150.3 12.1 all_gather.74
  178.6 30.7 %reduce-scatter.79.cloned.1.call-done = f32[80,1152]{1,0:T(8,128)} async-done(((f32[320,1152]{1,0:T(8,128)}), f32[80,1152]{1,0:T(8,128)}) %reduce-scatter.79.cloned.1.call-update) | async-done | bytes 368656
  211.3 11.5 all_gather.75
  222.8 5.4 fusion.15
  232.7 26.3 %reduce-scatter.81.cloned.1.call-done = f32[80,1152]{1,0:T(8,128)} async-done(((f32[320,1152]{1,0:T(8,128)}), f32[80,1152]{1,0:T(8,128)}) %reduce-scatter.81.cloned.1.call-update) | async-done | bytes 368656
  264.3 12.6 all_gather.76
  292.9 30.7 %reduce-scatter.83.cloned.1.call-done = f32[80,1152]{1,0:T(8,128)} async-done(((f32[320,1152]{1,0:T(8,128)}), f32[80,1152]{1,0:T(8,128)}) %reduce-scatter.83.cloned.1.call-update) | async-done | bytes 368656
  325.6 11.5 all_gather.77
  337.2 5.4 fusion.13
  347.3 26.0 %reduce-scatter.85.cloned.1.call-done = f32[80,1152]{1,0:T(8,128)} async-done(((f32[320,1152]{1,0:T(8,128)}), f32[80,1152]{1,0:T(8,128)}) %reduce-scatter.85.cloned.1.call-update) | async-done | bytes 368656
  379.7 12.1 all_gather.81
  394.8 10.0 all_gather.78
  430.2 17.9 %all_gather.80 = bf16[320,1152]{1,0:T(8,128)(2,1)} all-gather(bf16[80,1152]{1,0:T(8,128)(2,1)S(1)} %get-tuple-element.68), channel_id=1, replica_groups=mesh['section'=2,'dp'=4,'mp'=4] {'mp'}, dimensions={0}, use_global_device_ids=true | all-gather | bytes 921600 | tf_op jit(solution)/shard_map/all_gather | solution.py:49
  448.1 13.4 reduce-scatter.91.cloned.1.call-done
  463.5 11.0 all_gather.82
  483.1 30.6 %reduce-scatter.93.cloned.1.call-done = f32[80,1152]{1,0:T(8,128)} async-done(((f32[320,1152]{1,0:T(8,128)}), f32[80,1152]{1,0:T(8,128)}) %reduce-scatter.93.cloned.1.call-update) | async-done | bytes 368656
  518.9 11.1 all_gather.83
  537.5 30.6 %reduce-scatter.95.cloned.1.call-done = f32[80,1152]{1,0:T(8,128)} async-done(((f32[320,1152]{1,0:T(8,128)}), f32[80,1152]{1,0:T(8,128)}) %reduce-scatter.95.cloned.1.call-update) | async-done | bytes 368656
  572.1 11.0 all_gather.85
  607.8 15.9 %all_gather.84 = bf16[320,1152]{1,0:T(8,128)(2,1)} all-gather(bf16[80,1152]{1,0:T(8,128)(2,1)S(1)} %get-tuple-element.66), channel_id=1, replica_groups=mesh['section'=2,'dp'=4,'mp'=4] {'mp'}, dimensions={0}, use_global_device_ids=true | all-gather | bytes 921600 | tf_op jit(solution)/shard_map/all_gather | solution.py:49
  623.7 11.2 reduce-scatter.97.cloned.1.call-done
  637.0 11.0 all_gather.86
  656.7 30.7 %reduce-scatter.99.cloned.1.call-done = f32[80,1152]{1,0:T(8,128)} async-done(((f32[320,1152]{1,0:T(8,128)}), f32[80,1152]{1,0:T(8,128)}) %reduce-scatter.99.cloned.1.call-update) | async-done | bytes 368656
  692.6 11.1 all_gather.87
  720.6 21.2 %reduce-scatter.101.cloned.1.call-done = f32[80,1152]{1,0:T(8,128)} async-done(((f32[320,1152]{1,0:T(8,128)}), f32[80,1152]{1,0:T(8,128)}) %reduce-scatter.101.cloned.1.call-update) | async-done | bytes 368656
  745.3 16.1 %all_gather.89 = bf16[320,1152]{1,0:T(8,128)(2,1)S(1)} all-gather(bf16[80,1152]{1,0:T(8,128)(2,1)S(1)} %get-tuple-element.134), channel_id=1, replica_groups=mesh['section'=2,'dp'=4,'mp'=4] {'mp'}, dimensions={0}, use_global_device_ids=true | all-gather | bytes 921600 | tf_op jit(solution)/shard_map/all_gather | solution.py:36
  786.8 16.6 %all_gather.88 = bf16[320,1152]{1,0:T(8,128)(2,1)} all-gather(bf16[80,1152]{1,0:T(8,128)(2,1)S(1)} %get-tuple-element.70), channel_id=1, replica_groups=mesh['section'=2,'dp'=4,'mp'=4] {'mp'}, dimensions={0}, use_global_device_ids=true | all-gather | bytes 921600 | tf_op jit(solution)/shard_map/all_gather | solution.py:49
  803.3 11.8 reduce-scatter.103.cloned.1.call-done
  817.9 11.0 all_gather.90
  837.4 30.7 %reduce-scatter.105.cloned.1.call-done = f32[80,1152]{1,0:T(8,128)} async-done(((f32[320,1152]{1,0:T(8,128)}), f32[80,1152]{1,0:T(8,128)}) %reduce-scatter.105.cloned.1.call-update) | async-done | bytes 368656
  873.3 11.1 all_gather.91
  892.5 30.1 %reduce-scatter.107.cloned.1.call-done = f32[80,1152]{1,0:T(8,128)} async-done(((f32[320,1152]{1,0:T(8,128)}), f32[80,1152]{1,0:T(8,128)}) %reduce-scatter.107.cloned.1.call-update) | async-done | bytes 368656
  926.7 11.0 all_gather.93
  966.5 14.8 %all_gather.92 = bf16[320,1152]{1,0:T(8,128)(2,1)} all-gather(bf16[80,1152]{1,0:T(8,128)(2,1)S(1)} %get-tuple-element.72), channel_id=1, replica_groups=mesh['section'=2,'dp'=4,'mp'=4] {'mp'}, dimensions={0}, use_global_device_ids=true | all-gather | bytes 921600 | tf_op jit(solution)/shard_map/all_gather | solution.py:49
  981.4 9.1 reduce-scatter.109.cloned.1.call-done
  994.2 11.0 all_gather.94
  1014.3 5.7 fusion.136
  1029.8 15.6 %all_gather.79 = bf16[320,1152]{1,0:T(8,128)(2,1)} all-gather(bf16[80,1152]{1,0:T(8,128)(2,1)S(1)} %copy-done.162), channel_id=1, replica_groups=mesh['section'=2,'dp'=4,'mp'=4] {'mp'}, dimensions={0}, use_global_device_ids=true | all-gather | bytes 921600 | tf_op jit(solution)/shard_map/all_gather | solution.py:36
  1045.4 5.4 fusion.11
  1058.3 14.0 all_gather.95
  1093.1 6.5 copy.271
  1099.9 5.2 convolution_add_fusion.2
  1106.9 3.3 fusion.1
  1110.3 3.1 fusion.416
  1117.1 3.2 fusion
  1131.1 3.3 convolution_add_fusion.7
  1139.1 5.2 fusion.2
  1144.3 4.2 copy.270
  1166.0 3.4 pad.7.clone
  1169.5 7.0 reshape.837
  1176.5 3.3 pad.8
  1180.5 19.4 %all-reduce.25 = (f32[1,1152]{1,0:T(1,128)}, f32[1,4,639]{2,1,0:T(4,128)}) all-reduce(f32[1,1152]{1,0:T(1,128)S(1)} %broadcast_in_dim.326, f32[1,4,639]{2,1,0:T(4,128)S(1)} %slice_bitcast_fusion), channel_id=1, replica_groups=mesh['section'=2,'dp'=4,'mp'=4] {'dp'}, use_global_device_ids=true, to_apply=%region_122.123 | all-reduce | flops 3708 | bytes 29664 | tf_op jit(solution)/shard_map/psum | solution.py:363
  1204.7 38.4 %reduce-scatter.71.cloned.1.call-done = bf16[1152,288]{0,1:T(8,128)(2,1)} async-done(((bf16[1152,1152]{0,1:T(8,128)(2,1)}), bf16[1152,288]{0,1:T(8,128)(2,1)}) %reduce-scatter.71.cloned.1.call-update) | async-done | bytes 663568 | tf_op jit(solution)/shard_map/reduce_scatter | solution.py:358
  1245.4 52.4 %reduce-scatter.69.cloned.1.call-done = bf16[288,1152]{1,0:T(8,128)(2,1)} async-done(((bf16[1152,1152]{1,0:T(8,128)(2,1)}), bf16[288,1152]{1,0:T(8,128)(2,1)}) %reduce-scatter.69.cloned.1.call-update) | async-done | bytes 663568 | tf_op jit(solution)/shard_map/reduce_scatter | solution.py:355
  1300.1 30.8 %reduce-scatter.113.cloned.1.call-done = f32[80,1152]{1,0:T(8,128)} async-done(((f32[320,1152]{1,0:T(8,128)}), f32[80,1152]{1,0:T(8,128)}) %reduce-scatter.113.cloned.1.call-update) | async-done | bytes 368656
  1334.1 78.3 %all-reduce.24 = (f32[1,4,1152]{2,1,0:T(4,128)}, f32[1,1152]{1,0:T(1,128)}, f32[1,1152]{1,0:T(1,128)}) all-reduce(f32[1,4,1152]{2,1,0:T(4,128)S(1)} %fusion.296, f32[1,1152]{1,0:T(1,128)} %broadcast_in_dim.323, f32[1,1152]{1,0:T(1,128)} %broadcast_in_dim.329), channel_id=1, replica_groups=mesh['section'=2,'dp'=4,'mp'=4] {'dp','mp'}, use_global_device_ids=true, to_apply=%region_104.105 | all-reduce | flops 6912 | bytes 55296 | tf_op jit(solution)/shard_map/psum | solution.py:364
  (924 shorter events, 397.4 us)
Async XLA Ops:
  7.2 101.5 %copy-start = (bf16[1,1152,1152]{2,1,0:T(8,128)(2,1)S(1)}, bf16[1,1152,1152]{2,1,0:T(8,128)(2,1)}, u32[]{:S(2)}) copy-start(bf16[1,1152,1152]{2,1,0:T(8,128)(2,1)} %param.25) | copy-start | bytes 7962628
  7.2 88.2 %reduce-scatter.75.cloned.1.call-start = ((), (), s32[]{:S(2)}) async-start(), calls=%async_computation.29 | async-start | bytes 1843200
  64.4 80.5 %reduce-scatter.77.cloned.1.call-start = ((), (), s32[]{:S(2)}) async-start(), calls=%async_computation.30 | async-start | bytes 1843200
  96.6 17.6 %copy-start.38 = (f32[80,1152]{1,0:T(8,128)}, f32[80,1152]{1,0:T(8,128)S(1)}, u32[]{:S(2)}) copy-start(f32[80,1152]{1,0:T(8,128)S(1)} %get-tuple-element.116) | copy-start | bytes 1105924
  114.2 95.1 %reduce-scatter.79.cloned.1.call-start = ((), (), s32[]{:S(2)}) async-start(), calls=%async_computation.31 | async-start | bytes 1843200
  115.6 257.7 %copy-start.174 = (f32[1152]{0:T(1024)}, f32[1152]{0:T(1024)S(1)}, u32[]{:S(2)}) copy-start(f32[1152]{0:T(1024)S(1)} %reduce.13) | copy-start | bytes 13828
  146.0 16.5 %copy-start.20 = (bf16[1,1152,3,288]{1,3,2,0:T(8,128)(2,1)S(1)}, bf16[1,1152,3,288]{1,3,2,0:T(8,128)(2,1)}, u32[]{:S(2)}) copy-start(bf16[1,1152,3,288]{1,3,2,0:T(8,128)(2,1)} %param.21) | copy-start | bytes 5971972
  146.0 2.8 collective-permute-start
  178.5 80.4 %reduce-scatter.81.cloned.1.call-start = ((), (), s32[]{:S(2)}) async-start(), calls=%async_computation.32 | async-start | bytes 1843200
  228.3 95.3 %reduce-scatter.83.cloned.1.call-start = ((), (), s32[]{:S(2)}) async-start(), calls=%async_computation.33 | async-start | bytes 1843200
  260.1 2.6 collective-permute-start.1
  261.7 15.1 %copy-start.21 = (bf16[1,1152,3,288]{1,3,2,0:T(8,128)(2,1)S(1)}, bf16[1,1152,3,288]{1,3,2,0:T(8,128)(2,1)}, u32[]{:S(2)}) copy-start(bf16[1,1152,3,288]{1,3,2,0:T(8,128)(2,1)} %param.21) | copy-start | bytes 5971972
  292.9 80.4 %reduce-scatter.85.cloned.1.call-start = ((), (), s32[]{:S(2)}) async-start(), calls=%async_computation.34 | async-start | bytes 1843200
  342.6 118.9 %reduce-scatter.91.cloned.1.call-start = ((), (), s32[]{:S(2)}) async-start(), calls=%async_computation.37 | async-start | bytes 1843200
  374.5 2.6 collective-permute-start.2
  427.8 86.0 %reduce-scatter.93.cloned.1.call-start = ((), (), s32[]{:S(2)}) async-start(), calls=%async_computation.38 | async-start | bytes 1843200
  428.5 172.7 %copy-start.194 = (f32[80]{0:T(128)}, f32[80]{0:T(128)S(1)}, u32[]{:S(2)}) copy-start(f32[80]{0:T(128)S(1)} %compare_convert_fusion) | copy-start | bytes 964
  483.0 85.1 %reduce-scatter.95.cloned.1.call-start = ((), (), s32[]{:S(2)}) async-start(), calls=%async_computation.39 | async-start | bytes 1843200
  517.0 84.1 %copy-start.218 = (f32[80]{0:T(128)}, f32[80]{0:T(128)S(1)}, u32[]{:S(2)}) copy-start(f32[80]{0:T(128)S(1)} %negate_multiply_fusion.7) | copy-start | bytes 964
  537.4 97.5 %reduce-scatter.97.cloned.1.call-start = ((), (), s32[]{:S(2)}) async-start(), calls=%async_computation.40 | async-start | bytes 1843200
  568.1 15.0 %copy-start.24 = (bf16[1,1152,3,288]{1,3,2,0:T(8,128)(2,1)S(1)}, bf16[1,1152,3,288]{1,3,2,0:T(8,128)(2,1)}, u32[]{:S(2)}) copy-start(bf16[1,1152,3,288]{1,3,2,0:T(8,128)(2,1)} %param.21) | copy-start | bytes 5971972
  601.1 86.3 %reduce-scatter.99.cloned.1.call-start = ((), (), s32[]{:S(2)}) async-start(), calls=%async_computation.41 | async-start | bytes 1843200
  601.1 35.0 %copy-start.221 = (f32[80]{0:T(128)}, f32[80]{0:T(128)S(1)}, u32[]{:S(2)}) copy-start(f32[80]{0:T(128)S(1)} %negate_multiply_fusion.6) | copy-start | bytes 964
  602.5 3.5 collective-permute-start.3
  604.6 86.1 %copy-start.208 = (f32[80]{0:T(128)}, f32[80]{0:T(128)S(1)}, u32[]{:S(2)}) copy-start(f32[80]{0:T(128)S(1)} %compare_convert_fusion.1) | copy-start | bytes 964
  656.6 85.1 %reduce-scatter.101.cloned.1.call-start = ((), (), s32[]{:S(2)}) async-start(), calls=%async_computation.42 | async-start | bytes 1843200
  711.1 92.2 %reduce-scatter.87.cloned.1.call-start = ((), (), s32[]{:S(2)}) async-start(), calls=%async_computation.35 | async-start | bytes 1843200
  720.5 22.7 %copy-start.234 = (f32[80]{0:T(128)S(1)}, f32[80]{0:T(128)}, u32[]{:S(2)}) copy-start(f32[80]{0:T(128)} %copy-done.233) | copy-start | bytes 964
  720.5 94.6 %reduce-scatter.103.cloned.1.call-start = ((), (), s32[]{:S(2)}) async-start(), calls=%async_computation.43 | async-start | bytes 1843200
  741.7 19.6 %copy-start.26 = (bf16[1,1152,3,288]{1,3,2,0:T(8,128)(2,1)S(1)}, bf16[1,1152,3,288]{1,3,2,0:T(8,128)(2,1)}, u32[]{:S(2)}) copy-start(bf16[1,1152,3,288]{1,3,2,0:T(8,128)(2,1)} %param.21) | copy-start | bytes 5971972
  743.2 19.2 %copy-start.235 = (f32[80]{0:T(128)}, f32[80]{0:T(128)S(1)}, u32[]{:S(2)}) copy-start(f32[80]{0:T(128)S(1)} %get-tuple-element.32) | copy-start | bytes 964
  780.4 87.7 %reduce-scatter.105.cloned.1.call-start = ((), (), s32[]{:S(2)}) async-start(), calls=%async_computation.44 | async-start | bytes 1843200
  780.5 36.5 %copy-start.223 = (f32[80]{0:T(128)}, f32[80]{0:T(128)S(1)}, u32[]{:S(2)}) copy-start(f32[80]{0:T(128)S(1)} %negate_multiply_fusion.4) | copy-start | bytes 964
  781.7 3.3 collective-permute-start.4
  783.6 87.8 %copy-start.210 = (f32[80]{0:T(128)}, f32[80]{0:T(128)S(1)}, u32[]{:S(2)}) copy-start(f32[80]{0:T(128)S(1)} %compare_convert_fusion.2) | copy-start | bytes 964
  837.4 85.2 %reduce-scatter.107.cloned.1.call-start = ((), (), s32[]{:S(2)}) async-start(), calls=%async_computation.45 | async-start | bytes 1843200
  891.8 32.2 %copy-start.236 = (f32[80]{0:T(128)S(1)}, f32[80]{0:T(128)}, u32[]{:S(2)}) copy-start(f32[80]{0:T(128)} %copy-done.235) | copy-start | bytes 964
  891.9 98.6 %reduce-scatter.109.cloned.1.call-start = ((), (), s32[]{:S(2)}) async-start(), calls=%async_computation.46 | async-start | bytes 1843200
  892.5 45.1 %copy-start.192 = (f32[80]{0:T(128)}, f32[80]{0:T(128)S(1)}, u32[]{:S(2)}) copy-start(f32[80]{0:T(128)S(1)} %broadcast_multiply_fusion.1) | copy-start | bytes 964
  922.6 15.1 %copy-start.28 = (bf16[1,1152,3,288]{1,3,2,0:T(8,128)(2,1)S(1)}, bf16[1,1152,3,288]{1,3,2,0:T(8,128)(2,1)}, u32[]{:S(2)}) copy-start(bf16[1,1152,3,288]{1,3,2,0:T(8,128)(2,1)} %param.21) | copy-start | bytes 5971972
  924.1 14.7 %copy-start.229 = (f32[80]{0:T(128)}, f32[80]{0:T(128)S(1)}, u32[]{:S(2)}) copy-start(f32[80]{0:T(128)S(1)} %get-tuple-element.31) | copy-start | bytes 964
  924.1 14.6 %copy-start.212 = (f32[80]{0:T(128)}, f32[80]{0:T(128)S(1)}, u32[]{:S(2)}) copy-start(f32[80]{0:T(128)S(1)} %fusion.315) | copy-start | bytes 964
  958.0 94.4 %reduce-scatter.111.cloned.1.call-start = ((), (), s32[]{:S(2)}) async-start(), calls=%async_computation.47 | async-start | bytes 1843200
  961.5 3.3 collective-permute-start.5
  1013.8 134.7 %reduce-scatter.89.cloned.1.call-start = ((), (), s32[]{:S(2)}) async-start(), calls=%async_computation.36 | async-start | bytes 1843200
  1050.9 149.0 %reduce-scatter.73.cloned.1.call-start = ((), (), s32[]{:S(2)}) async-start(), calls=%async_computation.27 | async-start | bytes 1105920
  1054.9 18.3 %copy-start.50 = (f32[288,1152]{1,0:T(8,128)S(1)}, f32[288,1152]{1,0:T(8,128)}, u32[]{:S(2)}) copy-start(f32[288,1152]{1,0:T(8,128)} %convolution_add_fusion.18) | copy-start | bytes 3981316
  1054.9 18.3 %copy-start.122 = (bf16[4,72,320]{2,1,0:T(8,128)(2,1)S(1)}, bf16[4,72,320]{2,1,0:T(8,128)(2,1)}, u32[]{:S(2)}) copy-start(bf16[4,72,320]{2,1,0:T(8,128)(2,1)} %copy-done.121) | copy-start | bytes 552964
  1056.4 18.1 %copy-start.220 = (f32[80]{0:T(128)}, f32[80]{0:T(128)S(1)}, u32[]{:S(2)}) copy-start(f32[80]{0:T(128)S(1)} %negate_multiply_fusion.1) | copy-start | bytes 964
  1085.8 115.8 %all-reduce.28.cloned.1.call-start = ((), (), s32[]{:S(2)}) async-start(), calls=%async_computation.28 | async-start | bytes 3538944
  1099.6 143.5 %reduce-scatter.71.cloned.1.call-start = ((), (), s32[]{:S(2)}) async-start(), calls=%async_computation.26 | async-start | bytes 3317760 | tf_op jit(solution)/shard_map/reduce_scatter | solution.py:358
  1110.2 187.6 %reduce-scatter.69.cloned.1.call-start = ((), (), s32[]{:S(2)}) async-start(), calls=%async_computation.25 | async-start | bytes 3317760 | tf_op jit(solution)/shard_map/reduce_scatter | solution.py:355
  1120.3 210.6 %reduce-scatter.113.cloned.1.call-start = ((), (), s32[]{:S(2)}) async-start(), calls=%async_computation.48 | async-start | bytes 1843200
  1137.8 277.5 %reduce-scatter.67.cloned.1.call-start = ((), (), s32[]{:S(2)}) async-start(), calls=%async_computation.24 | async-start | bytes 3317760 | tf_op jit(solution)/shard_map/reduce_scatter | solution.py:346
  1245.4 85.5 %copy-start.193 = (f32[80]{0:T(128)S(1)}, f32[80]{0:T(128)}, u32[]{:S(2)}) copy-start(f32[80]{0:T(128)} %copy-done.192) | copy-start | bytes 964
  1245.4 86.7 %copy-start.230 = (f32[80]{0:T(128)S(1)}, f32[80]{0:T(128)}, u32[]{:S(2)}) copy-start(f32[80]{0:T(128)} %copy-done.229) | copy-start | bytes 964
  1245.4 86.7 %copy-start.213 = (f32[80]{0:T(128)S(1)}, f32[80]{0:T(128)}, u32[]{:S(2)}) copy-start(f32[80]{0:T(128)} %copy-done.212) | copy-start | bytes 964
  1245.4 88.6 %copy-start.186 = (f32[1,1152]{1,0:T(1,128)S(1)}, f32[1,1152]{1,0:T(1,128)}, u32[]{:S(2)}) copy-start(f32[1,1152]{1,0:T(1,128)} %reshape.828) | copy-start | bytes 13828
  1245.4 88.6 %copy-start.187 = (f32[1,1152]{1,0:T(1,128)S(1)}, f32[1,1152]{1,0:T(1,128)}, u32[]{:S(2)}) copy-start(f32[1,1152]{1,0:T(1,128)} %reshape.825) | copy-start | bytes 13828
  1245.4 88.6 %copy-start.188 = (f32[1,1152]{1,0:T(1,128)S(1)}, f32[1,1152]{1,0:T(1,128)}, u32[]{:S(2)}) copy-start(f32[1,1152]{1,0:T(1,128)} %reshape.826) | copy-start | bytes 13828
  1245.4 88.6 %copy-start.189 = (f32[1,1152]{1,0:T(1,128)S(1)}, f32[1,1152]{1,0:T(1,128)}, u32[]{:S(2)}) copy-start(f32[1,1152]{1,0:T(1,128)} %reshape.831) | copy-start | bytes 13828
  1245.4 88.6 %copy-start.190 = (f32[1,1152]{1,0:T(1,128)S(1)}, f32[1,1152]{1,0:T(1,128)}, u32[]{:S(2)}) copy-start(f32[1,1152]{1,0:T(1,128)} %reshape.829) | copy-start | bytes 13828
  1245.4 88.6 %copy-start.191 = (f32[1,1152]{1,0:T(1,128)S(1)}, f32[1,1152]{1,0:T(1,128)}, u32[]{:S(2)}) copy-start(f32[1,1152]{1,0:T(1,128)} %reshape.830) | copy-start | bytes 13828
  1245.4 167.5 %copy-start.151 = (bf16[80,1152]{1,0:T(8,128)(2,1)S(1)}, bf16[80,1152]{1,0:T(8,128)(2,1)}, u32[]{:S(2)}) copy-start(bf16[80,1152]{1,0:T(8,128)(2,1)} %copy-done.149) | copy-start | bytes 552964
  (209 other events, 503.0 us)
Sparse Core Ops, SparseCore 0:
  64.5 30.8 reduce-scatter.74
  114.3 30.5 reduce-scatter.76
  178.7 30.5 reduce-scatter.78
  228.4 30.5 reduce-scatter.80
  293.0 30.5 reduce-scatter.82
  342.7 30.5 reduce-scatter.84
  427.9 33.5 reduce-scatter.90
  483.2 30.5 reduce-scatter.92
  537.6 30.4 reduce-scatter.94
  601.2 33.7 reduce-scatter.96
  656.7 30.5 reduce-scatter.98
  711.2 30.4 reduce-scatter.100
  744.7 33.2 reduce-scatter.86
  780.8 34.3 reduce-scatter.102
  837.5 30.5 reduce-scatter.104
  892.0 30.5 reduce-scatter.106
  958.1 32.3 reduce-scatter.108
  1013.9 32.5 reduce-scatter.110
  1051.0 33.2 reduce-scatter.88
  1087.0 24.6 reduce-scatter.72
  1114.1 74.7 all-reduce.27
  1191.3 51.8 reduce-scatter.70
  1245.4 52.3 reduce-scatter.68
  1300.7 30.1 reduce-scatter.112
  1333.2 53.2 reduce-scatter.66
where the time goes:
time: 1440 us; the launch traced here: 1420 us
  waiting for transfers between devices  517 us (36%)
  blocking collectives  402 us (28%)
  local copies, waits for them, and re-layouts  175 us (12%)
  matrix products  173 us (12%)
  other arithmetic  121 us (8%)
  between operations  26.2 us (2%)
    unnamed x47, waiting for transfers between devices  419 us
    all_gather x16, blocking collectives, widen_rows(): return lax.all_gather(rows_low, 'mp', axis=0, tiled=True)  192 us
    all_gather x8, blocking collectives, grad_widen_rows(): return lax.all_gather(rows_low, 'mp', axis=0, tiled=True)  113 us
    unnamed x511, local copies, waits for them, and re-layouts  88.9 us
    psum x1, blocking collectives, local(): shared = lax.psum((totals[0], totals[4], totals[8]), ('dp', 'mp'))  78.3 us
    reduce_scatter x1, waiting for transfers between devices, local(): lax.psum_scatter(final_mlp_in.astype(jnp.bfloat16), 'dp', scatter_dimensi...  52.4 us
    reduce_scatter x1, waiting for transfers between devices, local(): lax.psum_scatter(final_mlp_out.astype(jnp.bfloat16), 'dp', scatter_dimens...  38.4 us
    dot_general x12, matrix products, narrow_rows(): jnp.dot(left, weight, preferred_element_type=jnp.float32)  35.6 us
  transfers between devices with their start and end apart: 31, of which 25 were waited for; matrix products, arithmetic and copies ran while one was open for 14% of the time, Pallas kernels for 0%

commit v1 on v0

--- a/solution.py
+++ b/solution.py
@@ -38,11 +38,11 @@
 
 def narrow_rows(left, weight):
     return lax.psum_scatter(
-        jnp.dot(left, weight, preferred_element_type=jnp.float32),
+        jnp.dot(left, weight, preferred_element_type=jnp.float32).astype(jnp.bfloat16),
         "mp",
         scatter_dimension=0,
         tiled=True,
-    )
+    ).astype(jnp.float32)
 
 
 def grad_widen_rows(rows_low):
@@ -51,11 +51,13 @@
 
 def grad_narrow_rows(left, weight):
     return lax.psum_scatter(
-        lax.dot_general(left, weight, (((1,), (1,)), ((), ())), preferred_element_type=jnp.float32),
+        lax.dot_general(
+            left, weight, (((1,), (1,)), ((), ())), preferred_element_type=jnp.float32
+        ).astype(jnp.bfloat16),
         "mp",
         scatter_dimension=0,
         tiled=True,
-    )
+    ).astype(jnp.float32)
 
 
 def attention_scores(queries, key_rows, bias_full, key_mask):
@@ -128,7 +130,7 @@
     return (output, kept)
 
 
-def layer_backward(tokens, length, time_token, layer_params, grad_out):
+def layer_backward(kept, layer_params, grad_out):
     (
         norm_rows,
         qkv_flat,
@@ -141,7 +143,6 @@
         mlp_out_bias,
         bias_full,
     ) = layer_params
-    _, kept = layer_forward(tokens, length, time_token, layer_params)
     (
         norm_pull,
         normed_full,
@@ -222,7 +223,6 @@
     )
     column_sums = jnp.sum(grad_project.astype(jnp.float32), axis=0)
     time_columns = jnp.concatenate([column_sums[:local_width], column_sums[2 * local_width :]])
-    time_grad = time_token.astype(jnp.float32)[:, None] * time_columns[None, :]
     grad_normed = grad_narrow_rows(grad_project, qkv_flat)
     grad_tokens_part, gain_grad, offset_grad = norm_pull(grad_normed)
     grad_tokens = grad_mixed + grad_tokens_part
@@ -230,7 +230,7 @@
     gradients = (
         norms_grad,
         qkv_grad,
-        time_grad,
+        time_columns,
         out_grad,
         out_bias_grad,
         mlp_in_grad,
@@ -245,16 +245,6 @@
 def write_slot(store, slot_index, value, active):
     previous = lax.dynamic_index_in_dim(store, slot_index, 0, keepdims=False)
     return lax.dynamic_update_index_in_dim(store, jnp.where(active, value, previous), slot_index, 0)
-
-
-def weight_members(totals, model_width, local_width):
-    return (
-        totals[1].reshape(model_width, 3, local_width),
-        totals[2].reshape(model_width, 2, local_width),
-        totals[3],
-        totals[5],
-        totals[7],
-    )
 
 
 def local(
@@ -304,7 +294,7 @@
         row_mask = (row_index < length).astype(jnp.float32)[:, None]
         return (length, time_token, row_mask)
 
-    kept_inputs = jnp.zeros((micro_total, row_count, model_width), jnp.bfloat16)
+    kept_ticks = []
     boundary = jnp.zeros((micro_total, row_count, model_width), jnp.float32)
     received = jnp.zeros((row_count, model_width), jnp.bfloat16)
     for tick_index in range(micro_total + 1):
@@ -313,12 +303,15 @@
         slot_index = jnp.clip(micro_index, 0, micro_total - 1)
         length, time_token, row_mask = image_inputs(slot_index)
         arriving = jnp.where(section_rank == 0, images[min(tick_index, micro_total - 1)], received)
-        output, _ = layer_forward(arriving.astype(jnp.float32), length, time_token, layer_params)
-        kept_inputs = write_slot(kept_inputs, slot_index, arriving, active)
+        output, kept = layer_forward(
+            arriving.astype(jnp.float32), length, time_token, layer_params
+        )
+        kept_ticks.append(kept)
         boundary = write_slot(boundary, slot_index, output * row_mask, active & (section_rank == 1))
         if tick_index < micro_total:
             received = from_behind(output.astype(jnp.bfloat16), "section", 1)
     totals = None
+    time_slots = jnp.zeros((micro_total, 2 * local_width), jnp.float32)
     incoming = jnp.zeros((row_count, model_width), jnp.bfloat16)
     for tick_index in range(micro_total + 1):
         micro_index = micro_total - tick_index - section_rank
@@ -328,10 +321,12 @@
         given_grad = cotangent[max(micro_total - 1 - tick_index, 0)].astype(jnp.float32) * row_mask
         grad_out = jnp.where(section_rank == 1, given_grad, incoming.astype(jnp.float32))
         grad_out = jnp.where(active, grad_out, 0.0)
-        tokens = lax.dynamic_index_in_dim(kept_inputs, slot_index, 0, keepdims=False).astype(
-            jnp.float32
+        grad_tokens, gradients = layer_backward(
+            kept_ticks[micro_total - tick_index], layer_params, grad_out
         )
-        grad_tokens, gradients = layer_backward(tokens, length, time_token, layer_params, grad_out)
+        columns = gradients[2]
+        gradients = gradients[:2] + (jnp.zeros((), jnp.float32),) + gradients[3:]
+        time_slots = write_slot(time_slots, slot_index, columns, active)
         if totals is None:
             totals = gradients
         else:
@@ -339,16 +334,26 @@
         boundary = write_slot(boundary, slot_index, grad_tokens, active & (section_rank == 0))
         if tick_index < micro_total:
             incoming = from_behind(grad_tokens.astype(jnp.bfloat16), "section", -1)
-    final_qkv, final_time, final_out, final_mlp_in, final_mlp_out = weight_members(
-        totals, model_width, local_width
-    )
+    final_qkv = totals[1].reshape(model_width, 3, local_width)
+    final_out, final_mlp_in, final_mlp_out = totals[3], totals[5], totals[7]
+    all_slots = lax.all_gather(time_slots, "dp", axis=0, tiled=True)
+    all_steps = lax.all_gather(timesteps, "dp", axis=0, tiled=True)
+    share = model_width // lax.axis_size("dp")
+    time_rows = lax.dynamic_slice_in_dim(
+        time_table[all_steps], lax.axis_index("dp") * share, share, axis=1
+    )
+    time_grad = lax.dot_general(
+        time_rows.astype(jnp.float32),
+        all_slots,
+        (((0,), (0,)), ((), ())),
+        precision=lax.Precision.HIGHEST,
+        preferred_element_type=jnp.float32,
+    ).reshape(share, 2, local_width)
     summed = (
         lax.psum_scatter(
             final_qkv.astype(jnp.bfloat16), "dp", scatter_dimension=0, tiled=True
         ).astype(jnp.float32),
-        lax.psum_scatter(
-            final_time.astype(jnp.bfloat16), "dp", scatter_dimension=0, tiled=True
-        ).astype(jnp.float32),
+        time_grad,
         lax.psum_scatter(
             final_out.astype(jnp.bfloat16), "dp", scatter_dimension=1, tiled=True
         ).astype(jnp.float32),

time: 1440 us -> 1050 us (0.73)
  waiting for transfers between devices: 517 us -> 330 us
  blocking collectives: 402 us -> 309 us
  local copies, waits for them, and re-layouts: 175 us -> 116 us
  matrix products: 173 us -> 148 us
  other arithmetic: 121 us -> 103 us
    all_gather x16 -> x8, blocking collectives: 192 us -> 93.4 us  [widen_rows(): return lax.all_gather(rows_low, 'mp', axis=0, tiled=True)]
    unnamed x47 -> x37, waiting for transfers between devices: 419 us -> 324 us
    reduce_scatter x1, waiting for transfers between devices: 52.4 us -> 0.01 us  [local(): lax.psum_scatter(final_mlp_in.astype(jnp.bfloat16), 'dp', scatter_dimensi...]
    reduce_scatter x1, waiting for transfers between devices: 38.4 us -> 0.01 us  [local(): lax.psum_scatter(final_mlp_out.astype(jnp.bfloat16), 'dp', scatter_dimens...]
    unnamed x511 -> x450, local copies, waits for them, and re-layouts: 88.9 us -> 57.9 us
    dot_general x12 -> x8, matrix products: 35.6 us -> 16.4 us  [narrow_rows(): jnp.dot(left, weight, preferred_element_type=jnp.float32)]
    reduce_sum x19 -> x8, other arithmetic: 23.6 us -> 7.9 us  [layer_norm(): centred = values - jnp.mean(values, axis=-1, keepdims=True)]
    slice x16 -> x8, local copies, waits for them, and re-layouts: 21.9 us -> 7.48 us  [layer_forward(): key_rows = linear[:, local_width:2 * local_width].astype(jnp.bfloat16)]
  transfers between devices with their start and end apart: 31 -> 26, of which waited for: 25 -> 20; matrix products, arithmetic and copies ran while one was open for 14% -> 14% of each run, Pallas kernels for 0% -> 0%
where the time goes in v1:
time: 1050 us; the launch traced here: 1040 us
  waiting for transfers between devices  330 us (31%)
  blocking collectives  309 us (29%)
  matrix products  148 us (14%)
  local copies, waits for them, and re-layouts  116 us (11%)
  other arithmetic  103 us (10%)
  between operations  26 us (2%)
    unnamed x37, waiting for transfers between devices  324 us
    all_gather x8, blocking collectives, grad_widen_rows(): return lax.all_gather(rows_low, 'mp', axis=0, tiled=True)  98.3 us
    all_gather x8, blocking collectives, widen_rows(): return lax.all_gather(rows_low, 'mp', axis=0, tiled=True)  93.4 us
    psum x1, blocking collectives, local(): shared = lax.psum((totals[0], totals[4], totals[8]), ('dp', 'mp'))  76.2 us
    unnamed x450, local copies, waits for them, and re-layouts  57.9 us
    reduce_sum x16, other arithmetic, layer_norm(): return centred * lax.rsqrt(spread + EPSILON) * norm_gain + offset  22.7 us
  transfers between devices with their start and end apart: 26, of which 20 were waited for; matrix products, arithmetic and copies ran while one was open for 14% of the time, Pallas kernels for 0%

profile of v1, /device:TPU:0, one launch (start us, length us, event | category | flops | bytes accessed | tf_op | source)
XLA Modules:
  0.0 1042.0 jit_solution(9754367133309999627)
XLA Ops:
  11.7 12.5 %all_gather.54 = bf16[320,1152]{1,0:T(8,128)(2,1)S(1)} all-gather(bf16[80,1152]{1,0:T(8,128)(2,1)S(1)} %fusion.121), channel_id=1, replica_groups=mesh['section'=2,'dp'=4,'mp'=4] {'mp'}, dimensions={0}, use_global_device_ids=true | all-gather | bytes 921600 | tf_op jit(solution)/shard_map/all_gather | solution.py:36
  24.1 2.9 fusion.237
  41.7 3.1 slice.189
  44.7 7.8 reshape.570
  53.9 2.3 fusion.233
  60.2 26.1 %reduce-scatter.63.cloned.1.call-done = bf16[80,1152]{1,0:T(8,128)(2,1)} async-done(((bf16[320,1152]{1,0:T(8,128)(2,1)}), bf16[80,1152]{1,0:T(8,128)(2,1)}) %reduce-scatter.63.cloned.1.call-update) | async-done | bytes 184336
  89.6 11.0 %all_gather.55 = bf16[320,1152]{1,0:T(8,128)(2,1)S(1)} all-gather(bf16[80,1152]{1,0:T(8,128)(2,1)S(1)} %add_convert_fusion.11), channel_id=1, replica_groups=mesh['section'=2,'dp'=4,'mp'=4] {'mp'}, dimensions={0}, use_global_device_ids=true | all-gather | bytes 921600 | tf_op jit(solution)/shard_map/all_gather | solution.py:36
  101.4 3.0 convolution_add_fusion.12
  105.5 2.3 convolution_convert_fusion.15
  111.7 22.3 %reduce-scatter.65.cloned.1.call-done = bf16[80,1152]{1,0:T(8,128)(2,1)} async-done(((bf16[320,1152]{1,0:T(8,128)(2,1)}), bf16[80,1152]{1,0:T(8,128)(2,1)}) %reduce-scatter.65.cloned.1.call-update) | async-done | bytes 184336
  138.3 12.1 %all_gather.56 = bf16[320,1152]{1,0:T(8,128)(2,1)S(1)} all-gather(bf16[80,1152]{1,0:T(8,128)(2,1)S(1)} %fusion.119), channel_id=1, replica_groups=mesh['section'=2,'dp'=4,'mp'=4] {'mp'}, dimensions={0}, use_global_device_ids=true | all-gather | bytes 921600 | tf_op jit(solution)/shard_map/all_gather | solution.py:36
  164.5 26.1 %reduce-scatter.67.cloned.1.call-done = bf16[80,1152]{1,0:T(8,128)(2,1)} async-done(((bf16[320,1152]{1,0:T(8,128)(2,1)}), bf16[80,1152]{1,0:T(8,128)(2,1)}) %reduce-scatter.67.cloned.1.call-update) | async-done | bytes 184336
  193.9 10.9 %all_gather.57 = bf16[320,1152]{1,0:T(8,128)(2,1)S(1)} all-gather(bf16[80,1152]{1,0:T(8,128)(2,1)S(1)} %add_convert_fusion.10), channel_id=1, replica_groups=mesh['section'=2,'dp'=4,'mp'=4] {'mp'}, dimensions={0}, use_global_device_ids=true | all-gather | bytes 921600 | tf_op jit(solution)/shard_map/all_gather | solution.py:36
  205.8 3.0 convolution_add_fusion.11
  216.0 22.4 %reduce-scatter.69.cloned.1.call-done = bf16[80,1152]{1,0:T(8,128)(2,1)} async-done(((bf16[320,1152]{1,0:T(8,128)(2,1)}), bf16[80,1152]{1,0:T(8,128)(2,1)}) %reduce-scatter.69.cloned.1.call-update) | async-done | bytes 184336
  243.7 12.6 %all_gather.58 = bf16[320,1152]{1,0:T(8,128)(2,1)S(1)} all-gather(bf16[80,1152]{1,0:T(8,128)(2,1)S(1)} %fusion.117), channel_id=1, replica_groups=mesh['section'=2,'dp'=4,'mp'=4] {'mp'}, dimensions={0}, use_global_device_ids=true | all-gather | bytes 921600 | tf_op jit(solution)/shard_map/all_gather | solution.py:36
  266.2 2.4 fusion.235
  272.8 26.1 %reduce-scatter.71.cloned.1.call-done = bf16[80,1152]{1,0:T(8,128)(2,1)} async-done(((bf16[320,1152]{1,0:T(8,128)(2,1)}), bf16[80,1152]{1,0:T(8,128)(2,1)}) %reduce-scatter.71.cloned.1.call-update) | async-done | bytes 184336
  302.2 11.0 %all_gather.59 = bf16[320,1152]{1,0:T(8,128)(2,1)S(1)} all-gather(bf16[80,1152]{1,0:T(8,128)(2,1)S(1)} %add_convert_fusion.9), channel_id=1, replica_groups=mesh['section'=2,'dp'=4,'mp'=4] {'mp'}, dimensions={0}, use_global_device_ids=true | all-gather | bytes 921600 | tf_op jit(solution)/shard_map/all_gather | solution.py:36
  314.1 3.0 convolution_add_fusion.10
  324.4 22.3 %reduce-scatter.73.cloned.1.call-done = bf16[80,1152]{1,0:T(8,128)(2,1)} async-done(((bf16[320,1152]{1,0:T(8,128)(2,1)}), bf16[80,1152]{1,0:T(8,128)(2,1)}) %reduce-scatter.73.cloned.1.call-update) | async-done | bytes 184336
  352.0 12.1 %all_gather.60 = bf16[320,1152]{1,0:T(8,128)(2,1)S(1)} all-gather(bf16[80,1152]{1,0:T(8,128)(2,1)S(1)} %fusion.115), channel_id=1, replica_groups=mesh['section'=2,'dp'=4,'mp'=4] {'mp'}, dimensions={0}, use_global_device_ids=true | all-gather | bytes 921600 | tf_op jit(solution)/shard_map/all_gather | solution.py:36
  372.0 2.4 fusion.236
  387.0 14.1 %all_gather.62 = bf16[320,1152]{1,0:T(8,128)(2,1)} all-gather(bf16[80,1152]{1,0:T(8,128)(2,1)S(1)} %get-tuple-element.57), channel_id=1, replica_groups=mesh['section'=2,'dp'=4,'mp'=4] {'mp'}, dimensions={0}, use_global_device_ids=true | all-gather | bytes 921600 | tf_op jit(solution)/shard_map/all_gather | solution.py:49
  401.2 11.3 %reduce-scatter.75.cloned.1.call-done = bf16[80,1152]{1,0:T(8,128)(2,1)} async-done(((bf16[320,1152]{1,0:T(8,128)(2,1)}), bf16[80,1152]{1,0:T(8,128)(2,1)}) %reduce-scatter.75.cloned.1.call-update) | async-done | bytes 184336
  415.8 11.2 %all_gather.61 = bf16[320,1152]{1,0:T(8,128)(2,1)S(1)} all-gather(bf16[80,1152]{1,0:T(8,128)(2,1)S(1)} %add_convert_fusion.8), channel_id=1, replica_groups=mesh['section'=2,'dp'=4,'mp'=4] {'mp'}, dimensions={0}, use_global_device_ids=true | all-gather | bytes 921600 | tf_op jit(solution)/shard_map/all_gather | solution.py:36
  427.8 3.0 convolution_add_fusion.9
  436.3 26.0 %reduce-scatter.79.cloned.1.call-done = bf16[80,1152]{1,0:T(8,128)(2,1)} async-done(((bf16[320,1152]{1,0:T(8,128)(2,1)}), bf16[80,1152]{1,0:T(8,128)(2,1)}) %reduce-scatter.79.cloned.1.call-update) | async-done | bytes 184336
  467.1 11.1 %all_gather.63 = bf16[320,1152]{1,0:T(8,128)(2,1)S(1)} all-gather(bf16[80,1152]{1,0:T(8,128)(2,1)S(1)} %get-tuple-element.66), channel_id=1, replica_groups=mesh['section'=2,'dp'=4,'mp'=4] {'mp'}, dimensions={0}, use_global_device_ids=true | all-gather | bytes 921600 | tf_op jit(solution)/shard_map/all_gather | solution.py:49
  486.1 26.1 %reduce-scatter.81.cloned.1.call-done = bf16[80,1152]{1,0:T(8,128)(2,1)} async-done(((bf16[320,1152]{1,0:T(8,128)(2,1)}), bf16[80,1152]{1,0:T(8,128)(2,1)}) %reduce-scatter.81.cloned.1.call-update) | async-done | bytes 184336
  521.9 11.9 %all_gather.64 = bf16[320,1152]{1,0:T(8,128)(2,1)S(1)} all-gather(bf16[80,1152]{1,0:T(8,128)(2,1)S(1)} %get-tuple-element.55), channel_id=1, replica_groups=mesh['section'=2,'dp'=4,'mp'=4] {'mp'}, dimensions={0}, use_global_device_ids=true | all-gather | bytes 921600 | tf_op jit(solution)/shard_map/all_gather | solution.py:49
  539.3 25.9 %reduce-scatter.83.cloned.1.call-done = bf16[80,1152]{1,0:T(8,128)(2,1)} async-done(((bf16[320,1152]{1,0:T(8,128)(2,1)}), bf16[80,1152]{1,0:T(8,128)(2,1)}) %reduce-scatter.83.cloned.1.call-update) | async-done | bytes 184336
  570.2 11.1 %all_gather.65 = bf16[320,1152]{1,0:T(8,128)(2,1)S(1)} all-gather(bf16[80,1152]{1,0:T(8,128)(2,1)S(1)} %get-tuple-element.63), channel_id=1, replica_groups=mesh['section'=2,'dp'=4,'mp'=4] {'mp'}, dimensions={0}, use_global_device_ids=true | all-gather | bytes 921600 | tf_op jit(solution)/shard_map/all_gather | solution.py:49
  589.2 26.1 %reduce-scatter.85.cloned.1.call-done = bf16[80,1152]{1,0:T(8,128)(2,1)} async-done(((bf16[320,1152]{1,0:T(8,128)(2,1)}), bf16[80,1152]{1,0:T(8,128)(2,1)}) %reduce-scatter.85.cloned.1.call-update) | async-done | bytes 184336
  625.0 11.8 %all_gather.66 = bf16[320,1152]{1,0:T(8,128)(2,1)S(1)} all-gather(bf16[80,1152]{1,0:T(8,128)(2,1)S(1)} %get-tuple-element.59), channel_id=1, replica_groups=mesh['section'=2,'dp'=4,'mp'=4] {'mp'}, dimensions={0}, use_global_device_ids=true | all-gather | bytes 921600 | tf_op jit(solution)/shard_map/all_gather | solution.py:49
  642.2 26.1 %reduce-scatter.87.cloned.1.call-done = bf16[80,1152]{1,0:T(8,128)(2,1)} async-done(((bf16[320,1152]{1,0:T(8,128)(2,1)}), bf16[80,1152]{1,0:T(8,128)(2,1)}) %reduce-scatter.87.cloned.1.call-update) | async-done | bytes 184336
  673.4 11.5 %all_gather.67 = bf16[320,1152]{1,0:T(8,128)(2,1)S(1)} all-gather(bf16[80,1152]{1,0:T(8,128)(2,1)S(1)} %get-tuple-element.69), channel_id=1, replica_groups=mesh['section'=2,'dp'=4,'mp'=4] {'mp'}, dimensions={0}, use_global_device_ids=true | all-gather | bytes 921600 | tf_op jit(solution)/shard_map/all_gather | solution.py:49
  692.8 26.1 %reduce-scatter.89.cloned.1.call-done = bf16[80,1152]{1,0:T(8,128)(2,1)} async-done(((bf16[320,1152]{1,0:T(8,128)(2,1)}), bf16[80,1152]{1,0:T(8,128)(2,1)}) %reduce-scatter.89.cloned.1.call-update) | async-done | bytes 184336
  728.5 12.4 %all_gather.68 = bf16[320,1152]{1,0:T(8,128)(2,1)S(1)} all-gather(bf16[80,1152]{1,0:T(8,128)(2,1)S(1)} %get-tuple-element.61), channel_id=1, replica_groups=mesh['section'=2,'dp'=4,'mp'=4] {'mp'}, dimensions={0}, use_global_device_ids=true | all-gather | bytes 921600 | tf_op jit(solution)/shard_map/all_gather | solution.py:49
  746.2 3.7 convolution_convert_fusion.12
  749.9 5.7 fusion.214
  760.8 11.5 %reduce-scatter.91.cloned.1.call-done = bf16[80,1152]{1,0:T(8,128)(2,1)} async-done(((bf16[320,1152]{1,0:T(8,128)(2,1)}), bf16[80,1152]{1,0:T(8,128)(2,1)}) %reduce-scatter.91.cloned.1.call-update) | async-done | bytes 184336
  777.8 14.4 %all_gather.69 = bf16[320,1152]{1,0:T(8,128)(2,1)S(1)} all-gather(bf16[80,1152]{1,0:T(8,128)(2,1)S(1)} %get-tuple-element.72), channel_id=1, replica_groups=mesh['section'=2,'dp'=4,'mp'=4] {'mp'}, dimensions={0}, use_global_device_ids=true | all-gather | bytes 921600 | tf_op jit(solution)/shard_map/all_gather | solution.py:49
  794.4 2.3 copy.90
  798.6 3.6 multiply_reduce_fusion
  802.3 5.2 convert_add_fusion
  812.9 5.3 convolution_add_fusion.2
  820.1 3.5 fusion.1
  825.7 8.4 all-reduce.3
  834.2 2.6 gather_fusion
  841.1 4.0 fusion.242
  847.9 4.6 convolution_add_fusion.5
  854.3 3.3 fusion
  859.0 4.4 fusion.213
  866.9 5.8 convolution_add_fusion.8
  877.2 3.9 convolution_add_fusion.7
  885.7 2.6 fusion.2
  888.3 4.2 copy.89
  894.2 14.0 %all-gather = f32[4,3,576]{2,1,0:T(4,128)S(1)} all-gather(f32[1,3,576]{2,1,0:T(4,128)S(1)} %dynamic_update_slice.51), channel_id=1, replica_groups=mesh['section'=2,'dp'=4,'mp'=4] {'dp'}, dimensions={0}, use_global_device_ids=true | all-gather | bytes 34560 | tf_op jit(solution)/shard_map/all_gather | solution.py:339
  910.3 3.5 pad.7
  913.8 7.0 reshape.615
  920.7 3.3 pad.8
  924.9 18.9 %all-reduce.21 = (f32[1,1152]{1,0:T(1,128)}, f32[1,4,639]{2,1,0:T(4,128)}) all-reduce(f32[1,1152]{1,0:T(1,128)S(1)} %copy-done.164, f32[1,4,639]{2,1,0:T(4,128)S(1)} %slice_bitcast_fusion), channel_id=1, replica_groups=mesh['section'=2,'dp'=4,'mp'=4] {'dp'}, use_global_device_ids=true, to_apply=%region_93.94 | all-reduce | flops 3708 | bytes 29664 | tf_op jit(solution)/shard_map/psum | solution.py:368
  950.0 76.2 %all-reduce.20 = (f32[1,4,1152]{2,1,0:T(4,128)}, f32[1,1152]{1,0:T(1,128)}, f32[1,1152]{1,0:T(1,128)}) all-reduce(f32[1,4,1152]{2,1,0:T(4,128)S(1)} %fusion.184, f32[1,1152]{1,0:T(1,128)S(1)} %copy-done.163, f32[1,1152]{1,0:T(1,128)S(1)} %copy-done.162), channel_id=1, replica_groups=mesh['section'=2,'dp'=4,'mp'=4] {'dp','mp'}, use_global_device_ids=true, to_apply=%region_76.77 | all-reduce | flops 6912 | bytes 55296 | tf_op jit(solution)/shard_map/psum | solution.py:369
  (770 shorter events, 269.4 us)
Async XLA Ops:
  7.2 98.4 %copy-start = (bf16[1,1152,1152]{2,1,0:T(8,128)(2,1)S(1)}, bf16[1,1152,1152]{2,1,0:T(8,128)(2,1)}, u32[]{:S(2)}) copy-start(bf16[1,1152,1152]{2,1,0:T(8,128)(2,1)} %param.27) | copy-start | bytes 7962628
  7.2 79.0 %reduce-scatter.63.cloned.1.call-start = ((), (), s32[]{:S(2)}) async-start(), calls=%async_computation.24 | async-start | bytes 921600
  8.5 18.5 %copy-start.165 = (f32[80]{0:T(128)}, f32[80]{0:T(128)S(1)}, u32[]{:S(2)}) copy-start(f32[80]{0:T(128)S(1)} %broadcast_multiply_fusion.7) | copy-start | bytes 964
  36.3 17.6 %copy-start.88 = (bf16[320,288]{0,1:T(8,128)(2,1)}, bf16[320,288]{0,1:T(8,128)(2,1)S(1)}, u32[]{:S(2)}) copy-start(bf16[320,288]{0,1:T(8,128)(2,1)S(1)} %copy.79) | copy-start | bytes 552964
  57.7 28.6 %copy-start.16 = (bf16[3,80,1152]{2,1,0:T(8,128)(2,1)S(1)}, bf16[3,80,1152]{2,1,0:T(8,128)(2,1)}, u32[]{:S(2)}) copy-start(bf16[3,80,1152]{2,1,0:T(8,128)(2,1)} %param.15) | copy-start | bytes 1658884
  59.8 74.2 %reduce-scatter.65.cloned.1.call-start = ((), (), s32[]{:S(2)}) async-start(), calls=%async_computation.25 | async-start | bytes 921600
  88.5 15.9 %copy-start.195 = (f32[80]{0:T(128)}, f32[80]{0:T(128)S(1)}, u32[]{:S(2)}) copy-start(f32[80]{0:T(128)S(1)} %multiply_reduce_fusion.7) | copy-start | bytes 964
  107.8 26.2 %copy-start.21 = (bf16[80,1152]{1,0:T(8,128)(2,1)S(1)}, bf16[80,1152]{1,0:T(8,128)(2,1)}, u32[]{:S(2)}) copy-start(bf16[80,1152]{1,0:T(8,128)(2,1)} %reduce-scatter.63.cloned.1.call-done) | copy-start | bytes 552964
  107.9 82.7 %reduce-scatter.67.cloned.1.call-start = ((), (), s32[]{:S(2)}) async-start(), calls=%async_computation.26 | async-start | bytes 921600
  134.0 16.5 %copy-start.207 = (bf16[1,1152,3,288]{1,3,2,0:T(8,128)(2,1)S(1)}, bf16[1,1152,3,288]{1,3,2,0:T(8,128)(2,1)}, u32[]{:S(2)}) copy-start(bf16[1,1152,3,288]{1,3,2,0:T(8,128)(2,1)} %param.21) | copy-start | bytes 5971972
  135.2 2.6 collective-permute-start
  162.5 30.4 %copy-start.84 = (bf16[4,72,320]{2,1,0:T(8,128)(2,1)}, bf16[4,72,320]{2,1,0:T(8,128)(2,1)S(1)}, u32[]{:S(2)}) copy-start(bf16[4,72,320]{2,1,0:T(8,128)(2,1)S(1)} %convolution_convert_fusion.26) | copy-start | bytes 552964
  164.5 73.9 %reduce-scatter.69.cloned.1.call-start = ((), (), s32[]{:S(2)}) async-start(), calls=%async_computation.27 | async-start | bytes 921600
  212.2 26.2 %copy-start.23 = (bf16[80,1152]{1,0:T(8,128)(2,1)S(1)}, bf16[80,1152]{1,0:T(8,128)(2,1)}, u32[]{:S(2)}) copy-start(bf16[80,1152]{1,0:T(8,128)(2,1)} %reduce-scatter.67.cloned.1.call-done) | copy-start | bytes 552964
  212.2 86.7 %reduce-scatter.71.cloned.1.call-start = ((), (), s32[]{:S(2)}) async-start(), calls=%async_computation.28 | async-start | bytes 921600
  238.4 17.9 %copy-start.208 = (bf16[1,1152,3,288]{1,3,2,0:T(8,128)(2,1)S(1)}, bf16[1,1152,3,288]{1,3,2,0:T(8,128)(2,1)}, u32[]{:S(2)}) copy-start(bf16[1,1152,3,288]{1,3,2,0:T(8,128)(2,1)} %param.21) | copy-start | bytes 5971972
  239.6 2.6 collective-permute-start.1
  272.8 73.9 %reduce-scatter.73.cloned.1.call-start = ((), (), s32[]{:S(2)}) async-start(), calls=%async_computation.29 | async-start | bytes 921600
  301.2 15.9 %copy-start.186 = (f32[80]{0:T(128)}, f32[80]{0:T(128)S(1)}, u32[]{:S(2)}) copy-start(f32[80]{0:T(128)S(1)} %fusion.206) | copy-start | bytes 964
  320.6 26.2 %copy-start.25 = (bf16[80,1152]{1,0:T(8,128)(2,1)S(1)}, bf16[80,1152]{1,0:T(8,128)(2,1)}, u32[]{:S(2)}) copy-start(bf16[80,1152]{1,0:T(8,128)(2,1)} %reduce-scatter.71.cloned.1.call-done) | copy-start | bytes 552964
  320.6 91.9 %reduce-scatter.75.cloned.1.call-start = ((), (), s32[]{:S(2)}) async-start(), calls=%async_computation.30 | async-start | bytes 921600
  346.7 17.4 %copy-start.209 = (bf16[1,1152,3,288]{1,3,2,0:T(8,128)(2,1)S(1)}, bf16[1,1152,3,288]{1,3,2,0:T(8,128)(2,1)}, u32[]{:S(2)}) copy-start(bf16[1,1152,3,288]{1,3,2,0:T(8,128)(2,1)} %param.21) | copy-start | bytes 5971972
  347.9 2.6 collective-permute-start.2
  384.6 77.7 %reduce-scatter.79.cloned.1.call-start = ((), (), s32[]{:S(2)}) async-start(), calls=%async_computation.32 | async-start | bytes 921600
  385.4 79.7 %copy-start.178 = (f32[80]{0:T(128)}, f32[80]{0:T(128)S(1)}, u32[]{:S(2)}) copy-start(f32[80]{0:T(128)S(1)} %compare_convert_fusion) | copy-start | bytes 964
  436.2 75.9 %reduce-scatter.81.cloned.1.call-start = ((), (), s32[]{:S(2)}) async-start(), calls=%async_computation.33 | async-start | bytes 921600
  486.0 79.2 %reduce-scatter.83.cloned.1.call-start = ((), (), s32[]{:S(2)}) async-start(), calls=%async_computation.34 | async-start | bytes 921600
  517.1 3.6 collective-permute-start.3
  519.2 48.8 %copy-start.182 = (f32[80]{0:T(128)}, f32[80]{0:T(128)S(1)}, u32[]{:S(2)}) copy-start(f32[80]{0:T(128)S(1)} %compare_convert_fusion.1) | copy-start | bytes 964
  536.9 29.5 %copy-start.187 = (f32[80]{0:T(128)S(1)}, f32[80]{0:T(128)}, u32[]{:S(2)}) copy-start(f32[80]{0:T(128)} %copy-done.186) | copy-start | bytes 964
  539.1 76.1 %reduce-scatter.85.cloned.1.call-start = ((), (), s32[]{:S(2)}) async-start(), calls=%async_computation.35 | async-start | bytes 921600
  587.2 29.2 %copy-start.202 = (f32[80]{0:T(128)S(1)}, f32[80]{0:T(128)}, u32[]{:S(2)}) copy-start(f32[80]{0:T(128)} %copy-done.201) | copy-start | bytes 964
  587.2 29.2 %copy-start.175 = (f32[80]{0:T(128)S(1)}, f32[80]{0:T(128)}, u32[]{:S(2)}) copy-start(f32[80]{0:T(128)} %copy-done.174) | copy-start | bytes 964
  589.1 79.2 %reduce-scatter.87.cloned.1.call-start = ((), (), s32[]{:S(2)}) async-start(), calls=%async_computation.36 | async-start | bytes 921600
  620.2 3.6 collective-permute-start.4
  622.2 49.1 %copy-start.184 = (f32[80]{0:T(128)}, f32[80]{0:T(128)S(1)}, u32[]{:S(2)}) copy-start(f32[80]{0:T(128)S(1)} %compare_convert_fusion.2) | copy-start | bytes 964
  640.0 29.4 %copy-start.200 = (f32[80]{0:T(128)S(1)}, f32[80]{0:T(128)}, u32[]{:S(2)}) copy-start(f32[80]{0:T(128)} %copy-done.199) | copy-start | bytes 964
  640.0 29.4 %copy-start.181 = (f32[80]{0:T(128)S(1)}, f32[80]{0:T(128)}, u32[]{:S(2)}) copy-start(f32[80]{0:T(128)} %copy-done.180) | copy-start | bytes 964
  642.2 76.7 %reduce-scatter.89.cloned.1.call-start = ((), (), s32[]{:S(2)}) async-start(), calls=%async_computation.37 | async-start | bytes 921600
  690.9 29.2 %copy-start.198 = (f32[80]{0:T(128)S(1)}, f32[80]{0:T(128)}, u32[]{:S(2)}) copy-start(f32[80]{0:T(128)} %copy-done.197) | copy-start | bytes 964
  692.8 79.5 %reduce-scatter.91.cloned.1.call-start = ((), (), s32[]{:S(2)}) async-start(), calls=%async_computation.38 | async-start | bytes 921600
  723.9 3.4 collective-permute-start.5
  746.2 99.8 %reduce-scatter.77.cloned.1.call-start = ((), (), s32[]{:S(2)}) async-start(), calls=%async_computation.31 | async-start | bytes 921600
  755.6 188.3 %reduce-scatter.61.cloned.1.call-start = ((), (), s32[]{:S(2)}) async-start(), calls=%async_computation.23 | async-start | bytes 1105920
  773.6 19.5 %copy-start.35 = (f32[288,1152]{1,0:T(8,128)S(1)}, f32[288,1152]{1,0:T(8,128)}, u32[]{:S(2)}) copy-start(f32[288,1152]{1,0:T(8,128)} %convolution_add_fusion.14) | copy-start | bytes 3981316
  773.6 19.5 %copy-start.83 = (bf16[4,72,320]{2,1,0:T(8,128)(2,1)S(1)}, bf16[4,72,320]{2,1,0:T(8,128)(2,1)}, u32[]{:S(2)}) copy-start(bf16[4,72,320]{2,1,0:T(8,128)(2,1)} %copy-done.82) | copy-start | bytes 552964
  802.2 145.1 %reduce-scatter.93.cloned.1.call-start = ((), (), s32[]{:S(2)}) async-start(), calls=%async_computation.39 | async-start | bytes 921600
  812.8 215.5 %reduce-scatter.59.cloned.1.call-start = ((), (), s32[]{:S(2)}) async-start(), calls=%async_computation.22 | async-start | bytes 3317760 | tf_op jit(solution)/shard_map/reduce_scatter | solution.py:363
  823.6 206.9 %reduce-scatter.57.cloned.1.call-start = ((), (), s32[]{:S(2)}) async-start(), calls=%async_computation.21 | async-start | bytes 3317760 | tf_op jit(solution)/shard_map/reduce_scatter | solution.py:360
  857.6 175.2 %reduce-scatter.55.cloned.1.call-start = ((), (), s32[]{:S(2)}) async-start(), calls=%async_computation.20 | async-start | bytes 3317760 | tf_op jit(solution)/shard_map/reduce_scatter | solution.py:353
  924.1 23.3 %copy-start.17 = (bf16[3,80,1152]{2,1,0:T(8,128)(2,1)S(1)}, bf16[3,80,1152]{2,1,0:T(8,128)(2,1)}, u32[]{:S(2)}) copy-start(bf16[3,80,1152]{2,1,0:T(8,128)(2,1)} %param.15) | copy-start | bytes 1658884
  924.1 23.3 %copy-start.166 = (f32[80]{0:T(128)S(1)}, f32[80]{0:T(128)}, u32[]{:S(2)}) copy-start(f32[80]{0:T(128)} %copy-done.165) | copy-start | bytes 964
  924.3 24.2 %copy-start.194 = (f32[80]{0:T(128)S(1)}, f32[80]{0:T(128)}, u32[]{:S(2)}) copy-start(f32[80]{0:T(128)} %copy-done.193) | copy-start | bytes 964
  924.3 24.2 %copy-start.177 = (f32[80]{0:T(128)S(1)}, f32[80]{0:T(128)}, u32[]{:S(2)}) copy-start(f32[80]{0:T(128)} %copy-done.176) | copy-start | bytes 964
  924.3 25.5 %copy-start.154 = (f32[1,1152]{1,0:T(1,128)S(1)}, f32[1,1152]{1,0:T(1,128)}, u32[]{:S(2)}) copy-start(f32[1,1152]{1,0:T(1,128)} %reshape.601) | copy-start | bytes 13828
  924.3 25.5 %copy-start.155 = (f32[1,1152]{1,0:T(1,128)S(1)}, f32[1,1152]{1,0:T(1,128)}, u32[]{:S(2)}) copy-start(f32[1,1152]{1,0:T(1,128)} %reshape.599) | copy-start | bytes 13828
  924.3 25.5 %copy-start.156 = (f32[1,1152]{1,0:T(1,128)S(1)}, f32[1,1152]{1,0:T(1,128)}, u32[]{:S(2)}) copy-start(f32[1,1152]{1,0:T(1,128)} %reshape.605) | copy-start | bytes 13828
  924.3 25.5 %copy-start.157 = (f32[1,1152]{1,0:T(1,128)S(1)}, f32[1,1152]{1,0:T(1,128)}, u32[]{:S(2)}) copy-start(f32[1,1152]{1,0:T(1,128)} %reshape.604) | copy-start | bytes 13828
  924.3 25.5 %copy-start.158 = (f32[1,1152]{1,0:T(1,128)S(1)}, f32[1,1152]{1,0:T(1,128)}, u32[]{:S(2)}) copy-start(f32[1,1152]{1,0:T(1,128)} %reshape.609) | copy-start | bytes 13828
  924.3 25.5 %copy-start.159 = (f32[1,1152]{1,0:T(1,128)S(1)}, f32[1,1152]{1,0:T(1,128)}, u32[]{:S(2)}) copy-start(f32[1,1152]{1,0:T(1,128)} %reshape.610) | copy-start | bytes 13828
  924.3 25.5 %copy-start.160 = (f32[1,1152]{1,0:T(1,128)S(1)}, f32[1,1152]{1,0:T(1,128)}, u32[]{:S(2)}) copy-start(f32[1,1152]{1,0:T(1,128)} %reshape.607) | copy-start | bytes 13828
  924.4 25.5 %copy-start.161 = (f32[1,1152]{1,0:T(1,128)S(1)}, f32[1,1152]{1,0:T(1,128)}, u32[]{:S(2)}) copy-start(f32[1,1152]{1,0:T(1,128)} %reshape.608) | copy-start | bytes 13828
  924.4 25.6 %copy-start.162 = (f32[1,1152]{1,0:T(1,128)S(1)}, f32[1,1152]{1,0:T(1,128)}, u32[]{:S(2)}) copy-start(f32[1,1152]{1,0:T(1,128)} %broadcast_in_dim.260) | copy-start | bytes 13828
  924.4 25.6 %copy-start.163 = (f32[1,1152]{1,0:T(1,128)S(1)}, f32[1,1152]{1,0:T(1,128)}, u32[]{:S(2)}) copy-start(f32[1,1152]{1,0:T(1,128)} %broadcast_in_dim.254) | copy-start | bytes 13828
  (177 other events, 653.9 us)
Sparse Core Ops, SparseCore 0:
  59.9 26.2 reduce-scatter.62
  108.0 25.9 reduce-scatter.64
  164.6 25.9 reduce-scatter.66
  212.3 26.0 reduce-scatter.68
  272.9 25.9 reduce-scatter.70
  320.7 25.9 reduce-scatter.72
  384.8 27.6 reduce-scatter.74
  436.3 25.9 reduce-scatter.78
  486.1 25.9 reduce-scatter.80
  539.2 25.9 reduce-scatter.82
  589.2 25.9 reduce-scatter.84
  642.3 25.9 reduce-scatter.86
  692.9 25.9 reduce-scatter.88
  746.3 25.9 reduce-scatter.90
  775.6 27.9 reduce-scatter.76
  805.8 24.7 reduce-scatter.60
  833.9 24.9 reduce-scatter.92
  861.1 53.2 reduce-scatter.58
  916.7 53.1 reduce-scatter.56
  972.0 52.6 reduce-scatter.54

commit v2 on v1

v2 whole, which is shorter than its diff:
```python
import functools
import math

import jax
import jax.numpy as jnp
from jax import lax
from jax.experimental import pallas as pl
from jax.experimental.pallas import tpu as pltpu
from jax.sharding import PartitionSpec as P

EPSILON = 1e-06
NEG_FILL = -1000000000.0
LANES = 128
BF = jnp.bfloat16
F32 = jnp.float32
ROOT = math.sqrt(2.0 / math.pi)
CUBIC = 0.044715


def mm(left, right, left_dim=1, right_dim=0):
    return lax.dot_general(
        left, right, (((left_dim,), (right_dim,)), ((), ())), preferred_element_type=F32
    )


def selection(rows, cols, head_size, flip):
    shape = (cols, rows) if flip else (rows, cols)
    row = lax.broadcasted_iota(jnp.int32, shape, 1 if flip else 0)
    col = lax.broadcasted_iota(jnp.int32, shape, 0 if flip else 1)
    within = col & (LANES - 1)
    hit = (within < head_size) & (row == (col // LANES) * head_size + within)
    return jnp.where(hit, 1.0, 0.0).astype(BF)


def normalize(values):
    centred = values - jnp.mean(values, axis=-1, keepdims=True)
    spread = jnp.mean(centred * centred, axis=-1, keepdims=True)
    scale = lax.rsqrt(spread + EPSILON)
    return centred * scale, scale


def norm_backward(grad, values, gain):
    unit, scale = normalize(values)
    inner = grad * gain
    mean_one = jnp.mean(inner, axis=-1, keepdims=True)
    mean_two = jnp.mean(inner * unit, axis=-1, keepdims=True)
    grad_in = scale * (inner - mean_one - unit * mean_two)
    gain_grad = jnp.sum(grad * unit, axis=0, keepdims=True)
    offset_grad = jnp.sum(grad, axis=0, keepdims=True)
    return grad_in, gain_grad, offset_grad


def layer_kernel(
    sizes,
    lengths_ref,
    images_ref,
    cotangent_ref,
    time_ref,
    norms_ref,
    qkv_raw_ref,
    out_w_ref,
    out_b_ref,
    in_w_ref,
    in_b_ref,
    back_w_ref,
    back_b_ref,
    table_ref,
    boundary_ref,
    small_ref,
    table_grad_ref,
    columns_ref,
    qkv_grad_ref,
    out_grad_ref,
    in_grad_ref,
    back_grad_ref,
    w_raw,
    w_qkv,
    w_out,
    w_in,
    w_back,
    normed,
    normed_two,
    grad_two,
    grad_one,
    active,
    grad_hidden,
    qkv,
    mixed_heads,
    grad_qkv,
    probs,
    slope,
    bias,
    score_sum,
    parts,
    sends,
    tokens,
    passed,
    mixed,
    stage,
    thin_stage,
    load_sem,
    gather_send,
    gather_recv,
    part_send,
    part_recv,
    pass_send,
    pass_recv,
    store_sem,
):
    n, count, rows, width, hidden_width, heads, head_size, shares = sizes
    seq = n * rows
    local = heads * head_size
    wide = heads * LANES
    share = width // shares
    score_scale = 1.0 / math.sqrt(head_size)
    me = lax.axis_index("mp")
    section = lax.axis_index("section")
    own = pl.multiple_of(me * rows, 16)

    def peer(d):
        return lax.rem(me + d, n)

    def source(d):
        return lax.rem(me + n - d, n)

    barrier = pltpu.get_barrier_semaphore()
    for d in range(1, n):
        pl.semaphore_signal(barrier, inc=1, device_id={"mp": peer(d)})
    pl.semaphore_signal(barrier, inc=1, device_id={"section": 1 - section})
    pl.semaphore_wait(barrier, n)

    loads = [
        pltpu.make_async_copy(a, b, load_sem.at[k])
        for k, (a, b) in enumerate(
            [(qkv_raw_ref, w_raw), (out_w_ref, w_out), (in_w_ref, w_in), (back_w_ref, w_back)]
        )
    ]
    for load in loads:
        load.start()

    def rows_of(i, index):
        return pl.ds(pl.multiple_of(i * seq + index * rows, 16), rows)

    def image_of(i):
        return pl.ds(pl.multiple_of(i * seq, 16), seq)

    def gather_copy(kind, buf, i, d, index):
        where = rows_of(i, index)
        return pltpu.make_async_remote_copy(
            src_ref=buf.at[where],
            dst_ref=buf.at[where],
            send_sem=gather_send.at[kind, i, d - 1],
            recv_sem=gather_recv.at[kind, i, d - 1],
            device_id={"mp": peer(d)},
        )

    def gather_start(kind, buf, i):
        for d in range(1, n):
            gather_copy(kind, buf, i, d, me).start()

    def gather_wait(kind, buf, i):
        for d in range(1, n):
            gather_copy(kind, buf, i, d, me).wait_send()
            gather_copy(kind, buf, i, d, source(d)).wait_recv()

    def part_copy(kind, i, d):
        return pltpu.make_async_remote_copy(
            src_ref=sends.at[rows_of(i, peer(d))],
            dst_ref=parts.at[kind & 1, i, d - 1],
            send_sem=part_send.at[kind, i, d - 1],
            recv_sem=part_recv.at[kind, i, d - 1],
            device_id={"mp": peer(d)},
        )

    def part_start(kind, i):
        for d in range(1, n):
            part_copy(kind, i, d).start()

    def part_sum(kind, i):
        for d in range(1, n):
            part_copy(kind, i, d).wait()
        total = sends[rows_of(i, me), :].astype(F32)
        for d in range(1, n):
            total = total + parts[kind & 1, i, d - 1].astype(F32)
        return total

    def pass_copy(k, i, dst):
        return pltpu.make_async_remote_copy(
            src_ref=passed.at[i],
            dst_ref=dst,
            send_sem=pass_send.at[k, i],
            recv_sem=pass_recv.at[k, i],
            device_id={"section": 1 - section},
        )

    def row_mask(i):
        index = me * rows + lax.broadcasted_iota(jnp.int32, (rows, 1), 0)
        return index < lengths_ref[i]

    def enter(i):
        @pl.when(section == 1)
        def _():
            pass_copy(0, i, tokens.at[i]).wait_recv()

        unit, _ = normalize(tokens[i].astype(F32))
        normed[rows_of(i, me), :] = (unit * norms_ref[0:1, :] + norms_ref[1:2, :]).astype(BF)
        gather_start(0, normed, i)

    def attend(i):
        gather_wait(0, normed, i)
        here = image_of(i)
        for j in range(3):
            linear = mm(normed[here, :], w_qkv[j])
            if j == 0:
                linear = linear + time_ref[i, 0:1, :]
            if j == 2:
                linear = linear + time_ref[i, 1:2, :]
            qkv[j, here, :] = linear.astype(BF)
        key_index = lax.broadcasted_iota(jnp.int32, (1, seq), 1)
        key_mask = key_index < lengths_ref[i]
        outs = []
        for h in range(heads):
            lanes = slice(h * LANES, (h + 1) * LANES)
            scores = mm(qkv[0, here, lanes], qkv[1, here, lanes], 1, 1) * score_scale + bias[h]
            scores = jnp.where(key_mask, scores, NEG_FILL)
            top = jnp.max(scores, axis=-1, keepdims=True)
            raised = jnp.exp(scores - top)
            prob = raised / jnp.sum(raised, axis=-1, keepdims=True)
            probs[i * heads + h] = prob
            outs.append(mm(prob.astype(BF), qkv[2, here, lanes]).astype(BF))
        packed = mm(jnp.concatenate(outs, axis=1), selection(local, wide, head_size, True))
        packed = packed.astype(BF)
        mixed_heads[here, :] = packed
        sends[here, :] = mm(packed, w_out[...]).astype(BF)
        part_start(0, i)

    def middle(i):
        total = tokens[i].astype(F32) + part_sum(0, i) + out_b_ref[...]
        mixed[i] = total
        unit, _ = normalize(total)
        normed_two[rows_of(i, me), :] = (unit * norms_ref[2:3, :] + norms_ref[3:4, :]).astype(BF)
        gather_start(1, normed_two, i)

    def feed(i):
        gather_wait(1, normed_two, i)
        here = image_of(i)
        hidden = mm(normed_two[here, :], w_in[...]) + in_b_ref[...]
        square = hidden * hidden
        bent = jnp.tanh(ROOT * (hidden + CUBIC * (square * hidden)))
        half = 0.5 * (1.0 + bent)
        active[here, :] = (hidden * half).astype(BF)
        slope[here, :] = half + 0.5 * hidden * (1.0 - bent * bent) * (
            ROOT + (3.0 * CUBIC * ROOT) * square
        )
        sends[here, :] = mm(active[here, :], w_back[...]).astype(BF)
        part_start(1, i)

    def leave(i):
        out = mixed[i] + part_sum(1, i) + back_b_ref[...]

        @pl.when(section == 0)
        def _():
            passed[i] = out.astype(BF)
            pass_copy(0, i, tokens.at[i]).start()

        @pl.when(section == 1)
        def _():
            boundary_ref[i] = jnp.where(row_mask(i), out, 0.0)

    def grad_enter(i):
        @pl.when(section == 0)
        def _():
            pass_copy(1, i, grad_two.at[rows_of(i, me)]).wait_recv()
            gather_start(2, grad_two, i)

    def feed_back(i):
        gather_wait(2, grad_two, i)
        here = image_of(i)
        grad_active = mm(grad_two[here, :], w_back[...], 1, 1)
        held = (slope[here, :] * grad_active).astype(BF)
        grad_hidden[here, :] = held
        small_ref[6:7, :] += jnp.sum(held.astype(F32), axis=0, keepdims=True)
        sends[here, :] = mm(held, w_in[...], 1, 1).astype(BF)
        part_start(2, i)

    def middle_back(i):
        grad = part_sum(2, i)
        grad_y = grad_two[rows_of(i, me), :].astype(F32)
        grad_in, gain, offset = norm_backward(grad, mixed[i], norms_ref[2:3, :])
        total = grad_y + grad_in
        mixed[i] = total
        low = total.astype(BF)
        grad_one[rows_of(i, me), :] = low
        gather_start(3, grad_one, i)
        small_ref[2:3, :] += gain
        small_ref[3:4, :] += offset
        small_ref[4:5, :] += jnp.sum(low.astype(F32), axis=0, keepdims=True)
        small_ref[5:6, :] += jnp.sum(grad_y, axis=0, keepdims=True)

    def attend_back(i):
        gather_wait(3, grad_one, i)
        here = image_of(i)
        grad_heads = mm(grad_one[here, :], w_out[...], 1, 1).astype(BF)
        grad_heads = mm(grad_heads, selection(local, wide, head_size, False)).astype(BF)
        outs = ([], [], [])
        for h in range(heads):
            lanes = slice(h * LANES, (h + 1) * LANES)
            grad_out = grad_heads[:, lanes]
            prob = probs[i * heads + h]
            grad_prob = mm(grad_out, qkv[2, here, lanes], 1, 1)
            outs[2].append(mm(prob.astype(BF), grad_out, 0, 0).astype(BF))
            inner = jnp.sum(prob * grad_prob, axis=-1, keepdims=True)
            grad_scores = (prob * (grad_prob - inner)).astype(BF)
            score_sum[h, :, 0:seq] += grad_scores.astype(F32)
            outs[0].append((mm(grad_scores, qkv[1, here, lanes]) * score_scale).astype(BF))
            outs[1].append((mm(grad_scores, qkv[0, here, lanes], 0, 0) * score_scale).astype(BF))
        total = None
        chosen = selection(local, wide, head_size, True)
        for j in range(3):
            grad = jnp.concatenate(outs[j], axis=1)
            term = mm(grad, w_qkv[j], 1, 1)
            total = term if total is None else total + term
            grad_qkv[j, here, :] = mm(grad, chosen).astype(BF)
            if j != 1:
                columns_ref[i, j // 2 : j // 2 + 1, :] = jnp.sum(
                    grad.astype(F32), axis=0, keepdims=True
                )
        sends[here, :] = total.astype(BF)
        part_start(3, i)

    def grad_leave(i):
        grad = part_sum(3, i)
        grad_in, gain, offset = norm_backward(grad, tokens[i].astype(F32), norms_ref[0:1, :])
        total = mixed[i] + grad_in

        @pl.when(section == 1)
        def _():
            passed[i] = total.astype(BF)
            pass_copy(1, i, grad_two.at[rows_of(i, me)]).start()

        @pl.when(section == 0)
        def _():
            boundary_ref[i] = total

        small_ref[0:1, :] += gain
        small_ref[1:2, :] += offset

    def each(body):
        def step(i, carry):
            body(i)
            return carry

        lax.fori_loop(0, count, step, 0)

    @pl.when(section == 0)
    def _():
        copy = pltpu.make_async_copy(images_ref, tokens, load_sem.at[4])
        copy.start()
        copy.wait()
        each(enter)

    @pl.when(section == 1)
    def _():
        def given(i):
            low = jnp.where(row_mask(i), cotangent_ref[i].astype(F32), 0.0).astype(BF)
            grad_two[rows_of(i, me), :] = low
            gather_start(2, grad_two, i)

        each(given)

    small_ref[...] = jnp.zeros_like(small_ref)
    score_sum[...] = jnp.zeros_like(score_sum)
    for h in range(heads):
        spread = jnp.broadcast_to(table_ref[h : h + 1, :], (seq, 2 * seq))
        bias[h] = pltpu.roll(spread, seq + 1, 1, stride=1, stride_axis=0)[:, :seq]
    loads[0].wait()
    chosen = selection(local, wide, head_size, False)
    for j in range(3):
        w_qkv[j] = mm(w_raw[j], chosen).astype(BF)
    for load in loads[1:]:
        load.wait()

    def forward(i):
        @pl.when(section == 1)
        def _():
            enter(i)

        attend(i)
        middle(i)
        feed(i)
        leave(i)

    each(forward)

    def backward(i):
        grad_enter(i)
        feed_back(i)
        middle_back(i)
        attend_back(i)
        grad_leave(i)

    each(backward)

    @pl.when(section == 0)
    def _():
        each(lambda i: pass_copy(0, i, tokens.at[i]).wait_send())

    @pl.when(section == 1)
    def _():
        each(lambda i: pass_copy(1, i, grad_two.at[rows_of(i, me)]).wait_send())

    lanes = 2 * seq
    carried = [jnp.zeros((8, lanes), F32) for _ in range(heads)]
    fill = jnp.zeros((8, lanes - score_sum.shape[2]), F32)

    def shift_add(g, carried):
        where = pl.ds(pl.multiple_of(g * 8, 8), 8)
        return [
            pltpu.roll(c, 8, 1) + jnp.concatenate([score_sum[h, where, :], fill], axis=1)
            for h, c in enumerate(carried)
        ]

    carried = lax.fori_loop(0, seq // 8, shift_add, carried)
    behind = 7 - lax.broadcasted_iota(jnp.int32, (8, lanes), 0)
    for h in range(heads):
        c = carried[h]
        for by in (1, 2, 4):
            c = jnp.where((behind & by) != 0, pltpu.roll(c, by, 1), c)
        table_grad_ref[h : h + 1, :] = jnp.sum(c, axis=0, keepdims=True)

    jobs = [
        (grad_two, active, back_grad_ref, None),
        (normed_two, grad_hidden, in_grad_ref, None),
        (grad_one, mixed_heads, out_grad_ref, None),
    ] + [(normed, grad_qkv.at[j], qkv_grad_ref, j) for j in range(3)]
    tile = width // 3
    for left, right, dst, j in jobs:
        cols = right.shape[1]

        def tile_step(t, carry, left=left, right=right, cols=cols):
            where = pl.ds(pl.multiple_of(t * tile, LANES), tile)
            slope[where, 0:cols] = mm(left[:, where], right[...], 0, 0)
            return carry

        lax.fori_loop(0, 3, tile_step, 0)

        def store(s, carry, dst=dst, j=j, cols=cols):
            where = pl.ds(pl.multiple_of(s * share, 8), share)
            target = dst.at[s] if j is None else dst.at[s, j]
            spot = stage if cols == stage.shape[1] else thin_stage
            spot[...] = slope[where, 0:cols].astype(BF)
            copy = pltpu.make_async_copy(spot, target, store_sem)
            copy.start()
            copy.wait()
            return carry

        lax.fori_loop(0, shares, store, 0)


def run_layer(sizes, args):
    n, count, rows, width, hidden_width, heads, head_size, shares = sizes
    seq = n * rows
    local_width = heads * head_size
    wide = heads * LANES
    share = width // shares
    total = count * seq
    vmem = pl.BlockSpec(memory_space=pltpu.VMEM)
    anywhere = pl.BlockSpec(memory_space=pl.ANY)
    dma = pltpu.SemaphoreType.DMA
    return pl.pallas_call(
        functools.partial(layer_kernel, sizes),
        out_shape=(
            jax.ShapeDtypeStruct((count, rows, width), F32),
            jax.ShapeDtypeStruct((8, width), F32),
            jax.ShapeDtypeStruct((heads, 2 * seq), F32),
            jax.ShapeDtypeStruct((count, 2, wide), F32),
            jax.ShapeDtypeStruct((shares, 3, share, local_width), BF),
            jax.ShapeDtypeStruct((shares, share, local_width), BF),
            jax.ShapeDtypeStruct((shares, share, hidden_width), BF),
            jax.ShapeDtypeStruct((shares, share, hidden_width), BF),
        ),
        in_specs=[
            pl.BlockSpec(memory_space=pltpu.SMEM),
            anywhere,
            vmem,
            vmem,
            vmem,
            anywhere,
            anywhere,
            vmem,
            anywhere,
            vmem,
            anywhere,
            vmem,
            vmem,
        ],
        out_specs=(vmem, vmem, vmem, vmem, anywhere, anywhere, anywhere, anywhere),
        scratch_shapes=[
            pltpu.VMEM((3, width, local_width), BF),
            pltpu.VMEM((3, width, wide), BF),
            pltpu.VMEM((local_width, width), BF),
            pltpu.VMEM((width, hidden_width), BF),
            pltpu.VMEM((hidden_width, width), BF),
            pltpu.VMEM((total, width), BF),
            pltpu.VMEM((total, width), BF),
            pltpu.VMEM((total, width), BF),
            pltpu.VMEM((total, width), BF),
            pltpu.VMEM((total, hidden_width), BF),
            pltpu.VMEM((total, hidden_width), BF),
            pltpu.VMEM((3, total, wide), BF),
            pltpu.VMEM((total, local_width), BF),
            pltpu.VMEM((3, total, local_width), BF),
            pltpu.VMEM((count * heads, seq, seq), F32),
            pltpu.VMEM((max(total, width), hidden_width), F32),
            pltpu.VMEM((heads, seq, seq), F32),
            pltpu.VMEM((heads, seq, -(-seq // LANES) * LANES), F32),
            pltpu.VMEM((2, count, n - 1, rows, width), BF),
            pltpu.VMEM((total, width), BF),
            pltpu.VMEM((count, rows, width), BF),
            pltpu.VMEM((count, rows, width), BF),
            pltpu.VMEM((count, rows, width), F32),
            pltpu.VMEM((share, hidden_width), BF),
            pltpu.VMEM((share, local_width), BF),
            dma((5,)),
            dma((4, count, n - 1)),
            dma((4, count, n - 1)),
            dma((4, count, n - 1)),
            dma((4, count, n - 1)),
            dma((2, count)),
            dma((2, count)),
            dma,
        ],
        compiler_params=pltpu.CompilerParams(
            collective_id=0, has_side_effects=True, vmem_limit_bytes=67043328
        ),
        name="two_pass",
    )(*args)


def local(
    images,
    cotangent,
    lengths,
    timesteps,
    time_table,
    norms,
    qkv_weight,
    time_weight,
    out_weight,
    out_bias,
    mlp_in_weight,
    mlp_in_bias,
    mlp_out_weight,
    mlp_out_bias,
    rel_bias,
):
    count, rows, width = images.shape
    local_width = qkv_weight.shape[3]
    hidden_width = mlp_in_weight.shape[2]
    heads = rel_bias.shape[1]
    head_size = local_width // heads
    shares = lax.axis_size("dp")
    share = width // shares
    sizes = (lax.axis_size("mp"), count, rows, width, hidden_width, heads, head_size, shares)
    time_rows = jnp.concatenate(
        [lax.dynamic_slice_in_dim(time_table, timesteps[i], 1, axis=0) for i in range(count)]
    )
    time_part = jnp.dot(
        time_rows, time_weight[0].reshape(width, 2 * local_width), preferred_element_type=F32
    ).reshape(count, 2, heads, head_size)
    time_part = jnp.pad(time_part, ((0, 0), (0, 0), (0, 0), (0, LANES - head_size)))
    time_part = time_part.reshape(count, 2, heads * LANES)
    table = jnp.pad(jnp.flip(rel_bias[0], axis=1), ((0, 0), (0, 1)))
    outs = run_layer(
        sizes,
        (
            lengths,
            images,
            cotangent,
            time_part,
            norms[0],
            jnp.transpose(qkv_weight[0], (1, 0, 2)),
            out_weight[0],
            out_bias,
            mlp_in_weight[0],
            mlp_in_bias,
            mlp_out_weight[0],
            mlp_out_bias,
            table,
        ),
    )
    boundary, small, table_grad, columns, qkv_grad, out_grad, in_grad, back_grad = outs
    columns = columns.reshape(count, 2, heads, LANES)[..., :head_size]
    columns = columns.reshape(count, 2 * local_width)
    all_columns = lax.all_gather(columns, "dp", axis=0, tiled=True)
    all_steps = lax.all_gather(timesteps, "dp", axis=0, tiled=True)
    all_rows = lax.dynamic_slice_in_dim(
        time_table[all_steps], lax.axis_index("dp") * share, share, axis=1
    )
    time_grad = lax.dot_general(
        all_rows.astype(F32),
        all_columns,
        (((0,), (0,)), ((), ())),
        precision=lax.Precision.HIGHEST,
        preferred_element_type=F32,
    ).reshape(share, 2, local_width)

    def scatter(value):
        return lax.psum_scatter(value, "dp", scatter_dimension=0).astype(F32)

    table_sum = lax.psum((jnp.flip(table_grad[:, : rel_bias.shape[2]], axis=1), small[6]), "dp")
    shared = lax.psum(small[:6], ("dp", "mp"))
    return (
        boundary[None],
        shared[None, :4],
        jnp.transpose(scatter(qkv_grad), (1, 0, 2))[None],
        time_grad[None],
        scatter(out_grad).T[None],
        shared[4][None],
        scatter(in_grad)[None],
        table_sum[1][None],
        scatter(back_grad).T[None],
        shared[5][None],
        table_sum[0][None],
    )


def solution(mesh):
    in_specs = (
        P("dp", "mp", None),
        P("dp", "mp", None),
        P("dp"),
        P("dp"),
        P(),
        P("section", None, None),
        P("section", None, None, "mp"),
        P("section", None, None, "mp"),
        P("section", "mp", None),
        P("section", None),
        P("section", None, "mp"),
        P("section", "mp"),
        P("section", "mp", None),
        P("section", None),
        P("section", "mp", None),
    )
    out_specs = (
        P("section", "dp", "mp", None),
        P("section", None, None),
        P("section", "dp", None, "mp"),
        P("section", "dp", None, "mp"),
        P("section", "mp", "dp"),
        P("section", None),
        P("section", "dp", "mp"),
        P("section", "mp"),
        P("section", "mp", "dp"),
        P("section", None),
        P("section", "mp", None),
    )
    return jax.shard_map(local, mesh=mesh, in_specs=in_specs, out_specs=out_specs, check_vma=False)
```

time: 1050 us -> 570 us (0.54)
  Pallas kernels: 0 us -> 347 us
  waiting for transfers between devices: 330 us -> 57.1 us
  blocking collectives: 309 us -> 118 us
  matrix products: 148 us -> 2.52 us
  local copies, waits for them, and re-layouts: 116 us -> 17 us
  other arithmetic: 103 us -> 7.69 us
    pallas_call x0 -> x1, Pallas kernels: none -> 347 us  [run_layer(): pl.pallas_call(functools.partial(layer_kernel, sizes), out_shape=(jax.Sha...]
    unnamed x37 -> x4, waiting for transfers between devices: 324 us -> 1.86 us
    all_gather x17 -> x1, blocking collectives: 206 us -> 13.3 us  [local(): all_columns = lax.all_gather(columns, 'dp', axis=0, tiled=True)]
    dot_general x77 -> x2, matrix products: 148 us -> 2.52 us  [the longest x1 1.93 us: local(): jnp.dot(time_rows, time_weight[0].reshape(width, 2 * local_width), prefer...]
    reduce_scatter x3 -> x4, waiting for transfers between devices: 0.01 us -> 55.2 us  [scatter(): return lax.psum_scatter(value, 'dp', scatter_dimension=0).astype(F32)]
    reduce_sum x49 -> x0, other arithmetic: 54.9 us -> none  [the longest x16 22.7 us: layer_norm(): return centred * lax.rsqrt(spread + EPSILON) * norm_gain + offset]
    unnamed x450 -> x26, local copies, waits for them, and re-layouts: 57.9 us -> 8.21 us
    convert_element_type x28 -> x1, other arithmetic: 25.6 us -> 2.24 us  [scatter(): return lax.psum_scatter(value, 'dp', scatter_dimension=0).astype(F32)]
  transfers between devices with their start and end apart: 26 -> 4, of which waited for: 20 -> 2; matrix products, arithmetic and copies ran while one was open for 14% -> 2% of each run, Pallas kernels for 0% -> 0%
where the time goes in v2:
time: 570 us; the launch traced here: 569 us
  Pallas kernels  347 us (61%)
  blocking collectives  118 us (21%)
  waiting for transfers between devices  57.1 us (10%)
  between operations  20.4 us (4%)
  local copies, waits for them, and re-layouts  17 us (3%)
  other arithmetic  7.69 us (1%)
    pallas_call x1, Pallas kernels, run_layer(): pl.pallas_call(functools.partial(layer_kernel, sizes), out_shape=(jax.Sha...  347 us
    psum x1, blocking collectives, local(): shared = lax.psum(small[:6], ('dp', 'mp'))  76.4 us
    reduce_scatter x4, waiting for transfers between devices, scatter(): return lax.psum_scatter(value, 'dp', scatter_dimension=0).astype(F32)  55.2 us
    psum x1, blocking collectives, local(): lax.psum((jnp.flip(table_grad[:, :rel_bias.shape[2]], axis=1), small[6]),...  18.9 us
    all_gather x1, blocking collectives, local(): all_columns = lax.all_gather(columns, 'dp', axis=0, tiled=True)  13.3 us
  transfers between devices with their start and end apart: 4, of which 2 were waited for; matrix products, arithmetic and copies ran while one was open for 2% of the time, Pallas kernels for 0%

profile of v2, /device:TPU:0, one launch (start us, length us, event | category | flops | bytes accessed | tf_op | source)
XLA Modules:
  0.0 568.9 jit_solution(9647479849803652956)
XLA Ops:
  7.2 0.0 reduce-scatter.7.cloned.1.call-start
  7.2 1.4 fusion.10
  14.4 0.8 constant_dynamic-slice_fusion.2
  15.2 1.9 fusion.2
  17.2 0.6 reshape.39.time_ref
  17.8 0.0 copy-start.3
  17.8 4.2 copy.33
  22.0 0.0 copy-done.3
  22.0 0.4 reverse
  22.4 0.1 slice.47
  22.5 0.6 pad.9.table_ref
  23.1 346.5 %two_pass.1 = (f32[3,80,1152]{2,1,0:T(8,128)}, f32[8,1152]{1,0:T(8,128)}, f32[4,640]{1,0:T(4,128)}, f32[3,2,512]{2,1,0:T(2,128)}, bf16[4,3,288,288]{3,2,1,0:T(8,...) custom-call(s32[3]{0:T(128)} %lengths_ref.1, ...), custom_call_target="tpu_custom_call" | custom-call | tf_op jit(solution)/shard_map/two_pass/pallas_call | solution.py:470
  369.6 0.0 reduce-scatter.7.cloned.1.call-update
  369.7 0.0 reduce-scatter.5.cloned.1.call-start
  369.7 0.7 reduce-scatter.5.cloned.1.call-update
  370.4 0.0 reduce-scatter.11.cloned.1.call-start
  370.5 0.7 reduce-scatter.11.cloned.1.call-update
  371.2 0.0 reduce-scatter.9.cloned.1.call-start
  371.2 0.0 copy-start.6
  371.2 0.0 copy-start.5
  371.2 0.0 copy-start.1
  371.2 0.0 copy-start.4
  371.2 0.0 copy-start.2
  371.3 0.5 reduce-scatter.9.cloned.1.call-update
  371.7 0.1 copy-done.6
  371.9 0.6 dynamic-slice
  373.1 0.0 copy-done.5
  373.1 0.2 dynamic-update-slice
  373.4 8.9 %all-reduce.2 = s32[12]{0:T(128)S(1)} all-reduce(s32[12]{0:T(128)S(1)} %dynamic-update-slice), channel_id=1, replica_groups=mesh['section'=2,'dp'=4,'mp'=4] {'dp'}, use_global_device_ids=true, to_apply=%add.2 | all-reduce | flops 12 | bytes 96
  382.3 0.0 copy-done.1
  382.3 0.0 copy-done.4
  382.3 0.5 reverse.1
  382.7 0.0 copy-done.2
  382.8 0.1 reshape.61
  382.9 13.3 %all-gather = f32[4,3,576]{2,1,0:T(4,128)S(1)} all-gather(f32[1,3,576]{2,1,0:T(4,128)S(1)} %reshape.61), channel_id=1, replica_groups=mesh['section'=2,'dp'=4,'mp'=4] {'dp'}, dimensions={0}, use_global_device_ids=true | all-gather | bytes 34560 | tf_op jit(solution)/shard_map/all_gather | solution.py:595
  396.2 2.6 gather_fusion
  398.8 0.6 fusion
  399.4 1.6 broadcast_in_dim_reshape.3
  400.9 0.1 slice_bitcast_fusion.1
  401.0 18.9 %all-reduce.3 = (f32[1,1152]{1,0:T(1,128)}, f32[1,4,639]{2,1,0:T(4,128)}) all-reduce(f32[1,1152]{1,0:T(1,128)S(1)} %slice.37, f32[1,4,639]{2,1,0:T(4,128)S(1)} %slice_bitcast_fusion.1), channel_id=1, replica_groups=mesh['section'=2,'dp'=4,'mp'=4] {'dp'}, use_global_device_ids=true, to_apply=%region_4.5 | all-reduce | flops 3708 | bytes 29664 | tf_op jit(solution)/shard_map/psum | solution.py:611
  419.9 76.4 %psum.21 = f32[6,1152]{1,0:T(8,128)S(1)} all-reduce(f32[6,1152]{1,0:T(8,128)S(1)} %bitcast.62), channel_id=1, replica_groups=mesh['section'=2,'dp'=4,'mp'=4] {'dp','mp'}, use_global_device_ids=true, to_apply=%region_0.1 | all-reduce | flops 6912 | bytes 55296 | tf_op jit(solution)/shard_map/psum | solution.py:612
  496.3 0.6 fusion.9
  496.9 0.6 slice_bitcast_fusion
  497.5 0.0 reduce-scatter.7.cloned.1.call-done
  497.5 1.0 convert_bitcast_fusion.2
  498.5 1.0 copy.34
  499.5 0.0 reduce-scatter.5.cloned.1.call-done
  499.5 2.2 convert_bitcast_fusion.1
  501.7 2.9 reduce-scatter.11.cloned.1.call-done
  504.6 2.2 convert_bitcast_fusion
  506.9 0.0 copy-start
  506.9 52.3 %reduce-scatter.9.cloned.1.call-done = bf16[1,288,1152]{2,1,0:T(8,128)(2,1)} async-done(((bf16[4,288,1152]{2,1,0:T(8,128)(2,1)}), bf16[1,288,1152]{2,1,0:T(8,128)(2,1)}) %reduce-scatter.9.cloned.1.call-update) | async-done | bytes 663568 | tf_op jit(solution)/shard_map/reduce_scatter | solution.py:609
  559.2 2.2 convert_element_type.23
  561.4 0.0 copy-done
  561.4 1.0 copy.39
  (8 shorter events, 0.1 us)
Async XLA Ops:
  7.2 490.4 %reduce-scatter.7.cloned.1.call-start = ((), (), s32[]{:S(2)}) async-start(), calls=%async_computation.5 | async-start | bytes 1105920 | tf_op jit(solution)/shard_map/reduce_scatter | solution.py:609
  17.8 4.2 copy-start.3
  369.7 129.8 %reduce-scatter.5.cloned.1.call-start = ((), (), s32[]{:S(2)}) async-start(), calls=%async_computation.4 | async-start | bytes 3317760 | tf_op jit(solution)/shard_map/reduce_scatter | solution.py:609
  370.4 134.2 %reduce-scatter.11.cloned.1.call-start = ((), (), s32[]{:S(2)}) async-start(), calls=%async_computation.7 | async-start | bytes 3317760 | tf_op jit(solution)/shard_map/reduce_scatter | solution.py:609
  371.2 188.0 %reduce-scatter.9.cloned.1.call-start = ((), (), s32[]{:S(2)}) async-start(), calls=%async_computation.6 | async-start | bytes 3317760 | tf_op jit(solution)/shard_map/reduce_scatter | solution.py:609
  371.2 0.7 copy-start.6
  371.2 1.9 copy-start.5
  371.2 11.0 %copy-start.1 = (f32[8,1152]{1,0:T(8,128)S(1)}, f32[8,1152]{1,0:T(8,128)}, u32[]{:S(2)}) copy-start(f32[8,1152]{1,0:T(8,128)} %get-tuple-element.20) | copy-start | bytes 110596
  371.2 11.0 %copy-start.4 = (f32[4,640]{1,0:T(4,128)S(1)}, f32[4,640]{1,0:T(4,128)}, u32[]{:S(2)}) copy-start(f32[4,640]{1,0:T(4,128)} %get-tuple-element.26) | copy-start | bytes 30724
  371.2 11.5 %copy-start.2 = (f32[3,2,512]{2,1,0:T(2,128)S(1)}, f32[3,2,512]{2,1,0:T(2,128)}, u32[]{:S(2)}) copy-start(f32[3,2,512]{2,1,0:T(2,128)} %get-tuple-element.22) | copy-start | bytes 36868
  506.9 54.5 %copy-start = (f32[3,80,1152]{2,1,0:T(8,128)S(1)}, f32[3,80,1152]{2,1,0:T(8,128)}, u32[]{:S(2)}) copy-start(f32[3,80,1152]{2,1,0:T(8,128)} %get-tuple-element.19) | copy-start | bytes 3317764
Sparse Core Ops, SparseCore 0:
  369.8 25.3 reduce-scatter.6
  397.5 52.0 reduce-scatter.4
  451.9 52.7 reduce-scatter.10
  506.8 52.3 reduce-scatter.8

commit v3 on v2

--- a/solution.py
+++ b/solution.py
@@ -65,10 +65,12 @@
     back_w_ref,
     back_b_ref,
     table_ref,
+    steps_ref,
     boundary_ref,
     small_ref,
     table_grad_ref,
     columns_ref,
+    rows_ref,
     qkv_grad_ref,
     out_grad_ref,
     in_grad_ref,
@@ -96,8 +98,9 @@
     tokens,
     passed,
     mixed,
-    stage,
-    thin_stage,
+    thin,
+    sums,
+    all_sums,
     load_sem,
     gather_send,
     gather_recv,
@@ -105,7 +108,13 @@
     part_recv,
     pass_send,
     pass_recv,
-    store_sem,
+    weight_send,
+    weight_recv,
+    weight_own,
+    tiny_send,
+    tiny_recv,
+    sum_send,
+    sum_recv,
 ):
     n, count, rows, width, hidden_width, heads, head_size, shares = sizes
     seq = n * rows
@@ -115,6 +124,7 @@
     score_scale = 1.0 / math.sqrt(head_size)
     me = lax.axis_index("mp")
     section = lax.axis_index("section")
+    replica = lax.axis_index("dp")
     own = pl.multiple_of(me * rows, 16)
 
     def peer(d):
@@ -127,7 +137,9 @@
     for d in range(1, n):
         pl.semaphore_signal(barrier, inc=1, device_id={"mp": peer(d)})
     pl.semaphore_signal(barrier, inc=1, device_id={"section": 1 - section})
-    pl.semaphore_wait(barrier, n)
+    for d in range(1, shares):
+        pl.semaphore_signal(barrier, inc=1, device_id={"dp": lax.rem(replica + d, shares)})
+    pl.semaphore_wait(barrier, n + shares - 1)
 
     loads = [
         pltpu.make_async_copy(a, b, load_sem.at[k])
@@ -279,7 +291,7 @@
         grad_active = mm(grad_two[here, :], w_back[...], 1, 1)
         held = (slope[here, :] * grad_active).astype(BF)
         grad_hidden[here, :] = held
-        small_ref[6:7, :] += jnp.sum(held.astype(F32), axis=0, keepdims=True)
+        sums[6:7, :] += jnp.sum(held.astype(F32), axis=0, keepdims=True)
         sends[here, :] = mm(held, w_in[...], 1, 1).astype(BF)
         part_start(2, i)
 
@@ -292,10 +304,10 @@
         low = total.astype(BF)
         grad_one[rows_of(i, me), :] = low
         gather_start(3, grad_one, i)
-        small_ref[2:3, :] += gain
-        small_ref[3:4, :] += offset
-        small_ref[4:5, :] += jnp.sum(low.astype(F32), axis=0, keepdims=True)
-        small_ref[5:6, :] += jnp.sum(grad_y, axis=0, keepdims=True)
+        sums[2:3, :] += gain
+        sums[3:4, :] += offset
+        sums[4:5, :] += jnp.sum(low.astype(F32), axis=0, keepdims=True)
+        sums[5:6, :] += jnp.sum(grad_y, axis=0, keepdims=True)
 
     def attend_back(i):
         gather_wait(3, grad_one, i)
@@ -322,7 +334,7 @@
             total = term if total is None else total + term
             grad_qkv[j, here, :] = mm(grad, chosen).astype(BF)
             if j != 1:
-                columns_ref[i, j // 2 : j // 2 + 1, :] = jnp.sum(
+                columns_ref[replica, i, j // 2 : j // 2 + 1, :] = jnp.sum(
                     grad.astype(F32), axis=0, keepdims=True
                 )
         sends[here, :] = total.astype(BF)
@@ -342,8 +354,8 @@
         def _():
             boundary_ref[i] = total
 
-        small_ref[0:1, :] += gain
-        small_ref[1:2, :] += offset
+        sums[0:1, :] += gain
+        sums[1:2, :] += offset
 
     def each(body):
         def step(i, carry):
@@ -368,7 +380,7 @@
 
         each(given)
 
-    small_ref[...] = jnp.zeros_like(small_ref)
+    sums[...] = jnp.zeros_like(sums)
     score_sum[...] = jnp.zeros_like(score_sum)
     for h in range(heads):
         spread = jnp.broadcast_to(table_ref[h : h + 1, :], (seq, 2 * seq))
@@ -380,26 +392,92 @@
     for load in loads[1:]:
         load.wait()
 
-    def forward(i):
+    def replica_peer(d):
+        return lax.rem(replica + d, shares)
+
+    def replica_source(d):
+        return lax.rem(replica + shares - d, shares)
+
+    def share_of(index):
+        return pl.ds(pl.multiple_of(index * share, 8), share)
+
+    def slot(array, index, j):
+        return array.at[index] if j is None else array.at[index, j]
+
+    jobs = [
+        (grad_two, active, w_back, back_grad_ref, None),
+        (normed_two, grad_hidden, w_in, in_grad_ref, None),
+        (grad_one, mixed_heads, thin, out_grad_ref, None),
+    ] + [(normed, grad_qkv.at[j], w_raw.at[j], qkv_grad_ref, j) for j in range(3)]
+    tile = width // 3
+
+    def own_copy(k):
+        _, _, buf, dst, j = jobs[k]
+        return pltpu.make_async_copy(
+            buf.at[share_of(replica)], slot(dst, replica, j), weight_own.at[k]
+        )
+
+    def weight_copy(k, d, index):
+        _, _, buf, dst, j = jobs[k]
+        return pltpu.make_async_remote_copy(
+            src_ref=buf.at[share_of(replica_peer(d))],
+            dst_ref=slot(dst, index, j),
+            send_sem=weight_send.at[k, d - 1],
+            recv_sem=weight_recv.at[k, d - 1],
+            device_id={"dp": replica_peer(d)},
+        )
+
+    def weight_job(k):
+        left, right, buf, _, _ = jobs[k]
+
+        def tile_step(t, carry):
+            where = pl.ds(pl.multiple_of(t * tile, LANES), tile)
+            buf[where, :] = mm(left[:, where], right[...], 0, 0).astype(BF)
+            return carry
+
+        lax.fori_loop(0, 3, tile_step, 0)
+        own_copy(k).start()
+        for d in range(1, shares):
+            weight_copy(k, d, replica).start()
+
+    def qkv_jobs(i):
+        for k in range(3, 6):
+            weight_job(k)
+
+    def later_enter(i):
         @pl.when(section == 1)
         def _():
             enter(i)
 
-        attend(i)
-        middle(i)
-        feed(i)
-        leave(i)
-
-    each(forward)
-
-    def backward(i):
-        grad_enter(i)
-        feed_back(i)
-        middle_back(i)
-        attend_back(i)
-        grad_leave(i)
-
-    each(backward)
+    schedule = (
+        (grad_enter, 11, 14, count),
+        (attend, 2, 2, count),
+        (middle, 3, 3, count),
+        (later_enter, 0, 0, count),
+        (leave, 6, 10, count),
+        (feed_back, 15, 10, count),
+        (grad_leave, 31, 17, count),
+        (feed, 4, 7, count),
+        (lambda i: weight_job(2), 31, 17, 1),
+        (qkv_jobs, 30, 19, 1),
+        (lambda i: weight_job(1), 17, 18, 1),
+        (middle_back, 23, 12, count),
+        (attend_back, 26, 14, count),
+        (lambda i: weight_job(0), 24, 19, 1),
+    )
+    steps = max(max(first, second) for _, first, second, _ in schedule) + count
+
+    def tick(t, carry):
+        for body, first, second, times in schedule:
+            i = t - (first + section * (second - first))
+
+            @pl.when((i >= 0) & (i < times))
+            def _(body=body, i=i):
+                body(i)
+
+        return carry
+
+    lax.fori_loop(0, steps, tick, 0)
 
     @pl.when(section == 0)
     def _():
@@ -408,6 +486,19 @@
     @pl.when(section == 1)
     def _():
         each(lambda i: pass_copy(1, i, grad_two.at[rows_of(i, me)]).wait_send())
+
+    def sum_copy(d, index):
+        return pltpu.make_async_remote_copy(
+            src_ref=all_sums.at[me],
+            dst_ref=all_sums.at[index],
+            send_sem=sum_send.at[d - 1],
+            recv_sem=sum_recv.at[d - 1],
+            device_id={"mp": peer(d)},
+        )
+
+    all_sums[me] = sums[...]
+    for d in range(1, n):
+        sum_copy(d, me).start()
 
     lanes = 2 * seq
     carried = [jnp.zeros((8, lanes), F32) for _ in range(heads)]
@@ -426,35 +517,41 @@
         c = carried[h]
         for by in (1, 2, 4):
             c = jnp.where((behind & by) != 0, pltpu.roll(c, by, 1), c)
-        table_grad_ref[h : h + 1, :] = jnp.sum(c, axis=0, keepdims=True)
-
-    jobs = [
-        (grad_two, active, back_grad_ref, None),
-        (normed_two, grad_hidden, in_grad_ref, None),
-        (grad_one, mixed_heads, out_grad_ref, None),
-    ] + [(normed, grad_qkv.at[j], qkv_grad_ref, j) for j in range(3)]
-    tile = width // 3
-    for left, right, dst, j in jobs:
-        cols = right.shape[1]
-
-        def tile_step(t, carry, left=left, right=right, cols=cols):
-            where = pl.ds(pl.multiple_of(t * tile, LANES), tile)
-            slope[where, 0:cols] = mm(left[:, where], right[...], 0, 0)
-            return carry
-
-        lax.fori_loop(0, 3, tile_step, 0)
-
-        def store(s, carry, dst=dst, j=j, cols=cols):
-            where = pl.ds(pl.multiple_of(s * share, 8), share)
-            target = dst.at[s] if j is None else dst.at[s, j]
-            spot = stage if cols == stage.shape[1] else thin_stage
-            spot[...] = slope[where, 0:cols].astype(BF)
-            copy = pltpu.make_async_copy(spot, target, store_sem)
-            copy.start()
-            copy.wait()
-            return carry
-
-        lax.fori_loop(0, shares, store, 0)
+        table_grad_ref[replica, h : h + 1, :] = jnp.sum(c, axis=0, keepdims=True)
+
+    for d in range(1, n):
+        sum_copy(d, me).wait_send()
+        sum_copy(d, source(d)).wait_recv()
+    total = all_sums[0]
+    for k in range(1, n):
+        total = total + all_sums[k]
+    kind = lax.broadcasted_iota(jnp.int32, (8, width), 0)
+    small_ref[replica] = jnp.where(kind < 6, total, sums[...])
+
+    tiny = (small_ref, table_grad_ref, columns_ref, rows_ref)
+
+    def tiny_copy(k, d, index):
+        return pltpu.make_async_remote_copy(
+            src_ref=tiny[k].at[replica],
+            dst_ref=tiny[k].at[index],
+            send_sem=tiny_send.at[k, d - 1],
+            recv_sem=tiny_recv.at[k, d - 1],
+            device_id={"dp": replica_peer(d)},
+        )
+
+    rows_ref[replica] = steps_ref[...]
+    for k in range(4):
+        for d in range(1, shares):
+            tiny_copy(k, d, replica).start()
+    for k in range(6):
+        own_copy(k).wait()
+        for d in range(1, shares):
+            weight_copy(k, d, replica).wait_send()
+            weight_copy(k, d, replica_source(d)).wait_recv()
+    for k in range(4):
+        for d in range(1, shares):
+            tiny_copy(k, d, replica).wait_send()
+            tiny_copy(k, d, replica_source(d)).wait_recv()
 
 
 def run_layer(sizes, args):
@@ -471,9 +568,10 @@
         functools.partial(layer_kernel, sizes),
         out_shape=(
             jax.ShapeDtypeStruct((count, rows, width), F32),
-            jax.ShapeDtypeStruct((8, width), F32),
-            jax.ShapeDtypeStruct((heads, 2 * seq), F32),
-            jax.ShapeDtypeStruct((count, 2, wide), F32),
+            jax.ShapeDtypeStruct((shares, 8, width), F32),
+            jax.ShapeDtypeStruct((shares, heads, 2 * seq), F32),
+            jax.ShapeDtypeStruct((shares, count, 2, wide), F32),
+            jax.ShapeDtypeStruct((shares, count, width), BF),
             jax.ShapeDtypeStruct((shares, 3, share, local_width), BF),
             jax.ShapeDtypeStruct((shares, share, local_width), BF),
             jax.ShapeDtypeStruct((shares, share, hidden_width), BF),
@@ -493,8 +591,9 @@
             anywhere,
             vmem,
             vmem,
+            vmem,
         ],
-        out_specs=(vmem, vmem, vmem, vmem, anywhere, anywhere, anywhere, anywhere),
+        out_specs=(vmem, vmem, vmem, vmem, vmem, anywhere, anywhere, anywhere, anywhere),
         scratch_shapes=[
             pltpu.VMEM((3, width, local_width), BF),
             pltpu.VMEM((3, width, wide), BF),
@@ -511,7 +610,7 @@
             pltpu.VMEM((total, local_width), BF),
             pltpu.VMEM((3, total, local_width), BF),
             pltpu.VMEM((count * heads, seq, seq), F32),
-            pltpu.VMEM((max(total, width), hidden_width), F32),
+            pltpu.VMEM((total, hidden_width), F32),
             pltpu.VMEM((heads, seq, seq), F32),
             pltpu.VMEM((heads, seq, -(-seq // LANES) * LANES), F32),
             pltpu.VMEM((2, count, n - 1, rows, width), BF),
@@ -519,8 +618,9 @@
             pltpu.VMEM((count, rows, width), BF),
             pltpu.VMEM((count, rows, width), BF),
             pltpu.VMEM((count, rows, width), F32),
-            pltpu.VMEM((share, hidden_width), BF),
-            pltpu.VMEM((share, local_width), BF),
+            pltpu.VMEM((width, local_width), BF),
+            pltpu.VMEM((8, width), F32),
+            pltpu.VMEM((n, 8, width), F32),
             dma((5,)),
             dma((4, count, n - 1)),
             dma((4, count, n - 1)),
@@ -528,7 +628,13 @@
             dma((4, count, n - 1)),
             dma((2, count)),
             dma((2, count)),
-            dma,
+            dma((6, shares - 1)),
+            dma((6, shares - 1)),
+            dma((6,)),
+            dma((4, shares - 1)),
+            dma((4, shares - 1)),
+            dma((n - 1,)),
+            dma((n - 1,)),
         ],
         compiler_params=pltpu.CompilerParams(
             collective_id=0, has_side_effects=True, vmem_limit_bytes=67043328
@@ -587,41 +693,40 @@
             mlp_out_weight[0],
             mlp_out_bias,
             table,
+            time_rows,
         ),
     )
-    boundary, small, table_grad, columns, qkv_grad, out_grad, in_grad, back_grad = outs
-    columns = columns.reshape(count, 2, heads, LANES)[..., :head_size]
-    columns = columns.reshape(count, 2 * local_width)
-    all_columns = lax.all_gather(columns, "dp", axis=0, tiled=True)
-    all_steps = lax.all_gather(timesteps, "dp", axis=0, tiled=True)
+    boundary, small, table_grad, columns, all_rows, qkv_grad, out_grad, in_grad, back_grad = outs
+    columns = columns.reshape(shares * count, 2, heads, LANES)[..., :head_size]
+    columns = columns.reshape(shares * count, 2 * local_width)
     all_rows = lax.dynamic_slice_in_dim(
-        time_table[all_steps], lax.axis_index("dp") * share, share, axis=1
+        all_rows.reshape(shares * count, width), lax.axis_index("dp") * share, share, axis=1
     )
     time_grad = lax.dot_general(
         all_rows.astype(F32),
-        all_columns,
+        columns,
         (((0,), (0,)), ((), ())),
         precision=lax.Precision.HIGHEST,
         preferred_element_type=F32,
     ).reshape(share, 2, local_width)
 
-    def scatter(value):
-        return lax.psum_scatter(value, "dp", scatter_dimension=0).astype(F32)
-
-    table_sum = lax.psum((jnp.flip(table_grad[:, : rel_bias.shape[2]], axis=1), small[6]), "dp")
-    shared = lax.psum(small[:6], ("dp", "mp"))
+    def added(value):
+        return jnp.sum(value.astype(F32), axis=0)
+
+    small = added(small)
+    table_grad = jnp.flip(added(table_grad)[:, : rel_bias.shape[2]], axis=1)
     return (
         boundary[None],
-        shared[None, :4],
-        jnp.transpose(scatter(qkv_grad), (1, 0, 2))[None],
+        small[None, :4],
+        jnp.transpose(added(qkv_grad), (1, 0, 2))[None],
         time_grad[None],
-        scatter(out_grad).T[None],
-        shared[4][None],
-        scatter(in_grad)[None],
-        table_sum[1][None],
-        scatter(back_grad).T[None],
-        shared[5][None],
-        table_sum[0][None],
+        added(out_grad).T[None],
+        small[4][None],
+        added(in_grad)[None],
+        small[6][None],
+        added(back_grad).T[None],
+        small[5][None],
+        table_grad[None],
     )
 
 

time: 570 us -> 380 us (0.67)
  blocking collectives: 118 us -> 0 us
  waiting for transfers between devices: 57.1 us -> 0 us
  between operations: 20.4 us -> 6.57 us
    psum x2 -> x0, blocking collectives: 95.3 us -> none  [the longest x1 76.4 us: local(): shared = lax.psum(small[:6], ('dp', 'mp'))]
    reduce_scatter x4 -> x0, waiting for transfers between devices: 55.2 us -> none  [scatter(): return lax.psum_scatter(value, 'dp', scatter_dimension=0).astype(F32)]
    all_gather x1 -> x0, blocking collectives: 13.3 us -> none  [local(): all_columns = lax.all_gather(columns, 'dp', axis=0, tiled=True)]
    unnamed x1 -> x0, blocking collectives: 8.9 us -> none
    reduce_sum x0 -> x5, other arithmetic: none -> 6.75 us  [added(): return jnp.sum(value.astype(F32), axis=0)]
  transfers between devices with their start and end apart: 4 -> 0, of which waited for: 2 -> 0; matrix products, arithmetic and copies ran while one was open for 2% -> 0% of each run, Pallas kernels for 0% -> 0%
where the time goes in v3:
time: 380 us; the launch traced here: 379 us
  Pallas kernels  348 us (92%)
  local copies, waits for them, and re-layouts  14.9 us (4%)
  other arithmetic  6.77 us (2%)
  between operations  6.57 us (2%)
    pallas_call x1, Pallas kernels, run_layer(): pl.pallas_call(functools.partial(layer_kernel, sizes), out_shape=(jax.Sha...  348 us
    unnamed x26, local copies, waits for them, and re-layouts  9.37 us

profile of v3, /device:TPU:0, one launch (start us, length us, event | category | flops | bytes accessed | tf_op | source)
XLA Modules:
  0.0 379.2 jit_solution(11266229441874972131)
XLA Ops:
  0.6 1.4 fusion.7
  7.8 0.8 constant_dynamic-slice_fusion.2
  8.6 0.0 copy-start.4
  8.6 0.6 copy-done.4
  9.2 1.9 fusion.3
  11.2 0.6 reshape.41.time_ref
  11.8 0.0 copy-start.8
  11.8 4.2 %copy.34 = bf16[1,1152,3,288]{3,1,2,0:T(8,128)(2,1)} copy(bf16[1,1152,3,288]{1,3,2,0:T(8,128)(2,1)} %param.21) | data formatting | bytes 3981312 | tf_op args[6]
  16.0 0.0 copy-done.8
  16.0 0.4 reverse
  16.5 0.1 slice.43
  16.6 0.6 pad.9.table_ref
  17.2 348.4 %two_pass.1 = (f32[3,80,1152]{2,1,0:T(8,128)}, f32[4,8,1152]{2,1,0:T(8,128)}, f32[4,4,640]{2,1,0:T(4,128)}, f32[4,3,2,512]{3,2,1,0:T(2,128)}, bf16[4,3,1152]{2,1...) custom-call(s32[3]{0:T(128)} %lengths_ref.1, ...), custom_call_target="tpu_custom_call" | custom-call | tf_op jit(solution)/shard_map/two_pass/pallas_call | solution.py:567
  365.5 0.0 copy-start.5
  365.6 0.0 copy-start.7
  365.6 5.1 %convert_reduce_fusion = (f32[288,1152]{1,0:T(8,128)}, f32[288,1152]{1,0:T(8,128)}) fusion(bf16[4,288,1152]{2,1,0:T(8,128)(2,1)} %get-tuple-element.27, bf16[4,288,1152]{2,1,0:T(8,128)(2,1)} %get-tuple-element.26), kind=kLoop, calls=%fused_computation | loop fusion | flops 4644864 | bytes 7962624 | tf_op jit(solution)/shard_map/reduce_sum | solution.py:714
  370.6 0.0 copy-start
  370.6 0.0 copy-done.5
  370.7 0.1 reshape.44
  370.8 0.1 dot_general.20
  370.9 0.0 copy-done.7
  370.9 0.6 convolution_bitcast_fusion
  371.6 1.6 copy.36
  373.2 0.0 copy-start.2
  373.2 0.0 copy-done
  373.2 0.0 copy-start.3
  373.2 0.0 copy-start.6
  373.2 1.5 convert_reduce_fusion.2
  374.7 0.0 copy-start.1
  374.7 0.0 copy-done.2
  374.7 0.1 convert_reduce_fusion.3
  374.9 1.0 copy.37
  375.8 0.0 copy-done.3
  375.8 0.6 slice_bitcast_fusion
  376.5 0.6 fusion.6
  377.1 0.0 copy-done.6
  377.1 0.5 reverse.1
  377.5 0.7 slice_bitcast_fusion.1
  378.2 0.0 copy-done.1
  378.2 1.0 copy.43
  (7 shorter events, 0.2 us)
Async XLA Ops:
  8.6 0.6 copy-start.4
  11.8 4.2 %copy-start.8 = (f32[1,4,639]{2,1,0:T(4,128)S(1)}, f32[1,4,639]{2,1,0:T(4,128)}, u32[]{:S(2)}) copy-start(f32[1,4,639]{2,1,0:T(4,128)} %param.29) | copy-start | bytes 30676
  365.5 5.1 %copy-start.5 = (f32[4,3,2,512]{3,2,1,0:T(2,128)S(1)}, f32[4,3,2,512]{3,2,1,0:T(2,128)}, u32[]{:S(2)}) copy-start(f32[4,3,2,512]{3,2,1,0:T(2,128)} %get-tuple-element.24) | copy-start | bytes 147460
  365.6 5.3 %copy-start.7 = (bf16[4,3,1152]{2,1,0:T(4,128)(2,1)S(1)}, bf16[4,3,1152]{2,1,0:T(4,128)(2,1)}, u32[]{:S(2)}) copy-start(bf16[4,3,1152]{2,1,0:T(4,128)(2,1)} %get-tuple-element.23) | copy-start | bytes 82948
  370.6 2.5 copy-start
  373.2 1.5 copy-start.2
  373.2 2.6 copy-start.3
  373.2 3.9 %copy-start.6 = (f32[4,4,640]{2,1,0:T(4,128)S(1)}, f32[4,4,640]{2,1,0:T(4,128)}, u32[]{:S(2)}) copy-start(f32[4,4,640]{2,1,0:T(4,128)} %get-tuple-element.28) | copy-start | bytes 122884
  374.7 3.5 copy-start.1

commit v4 on v3

--- a/solution.py
+++ b/solution.py
@@ -23,12 +23,12 @@
     )
 
 
-def selection(rows, cols, head_size, flip):
+def selection(rows, cols, head_size, flip, first=0):
     shape = (cols, rows) if flip else (rows, cols)
     row = lax.broadcasted_iota(jnp.int32, shape, 1 if flip else 0)
     col = lax.broadcasted_iota(jnp.int32, shape, 0 if flip else 1)
     within = col & (LANES - 1)
-    hit = (within < head_size) & (row == (col // LANES) * head_size + within)
+    hit = (within < head_size) & (row - first == (col // LANES) * head_size + within)
     return jnp.where(hit, 1.0, 0.0).astype(BF)
 
 
@@ -71,8 +71,7 @@
     table_grad_ref,
     columns_ref,
     rows_ref,
-    qkv_grad_ref,
-    out_grad_ref,
+    thin_grad_ref,
     in_grad_ref,
     back_grad_ref,
     w_raw,
@@ -98,7 +97,7 @@
     tokens,
     passed,
     mixed,
-    thin,
+    crossed,
     sums,
     all_sums,
     load_sem,
@@ -128,10 +127,12 @@
     own = pl.multiple_of(me * rows, 16)
 
     def peer(d):
+        if n == 4:
+            return (n - 1 - me, me + 1 - 2 * lax.rem(me, 2), lax.rem(me + 2, n))[d - 1]
         return lax.rem(me + d, n)
 
     def source(d):
-        return lax.rem(me + n - d, n)
+        return peer(d) if n == 4 else lax.rem(me + n - d, n)
 
     barrier = pltpu.get_barrier_semaphore()
     for d in range(1, n):
@@ -373,8 +374,12 @@
 
     @pl.when(section == 1)
     def _():
+        copy = pltpu.make_async_copy(cotangent_ref, passed, load_sem.at[4])
+        copy.start()
+        copy.wait()
+
         def given(i):
-            low = jnp.where(row_mask(i), cotangent_ref[i].astype(F32), 0.0).astype(BF)
+            low = jnp.where(row_mask(i), passed[i].astype(F32), 0.0).astype(BF)
             grad_two[rows_of(i, me), :] = low
             gather_start(2, grad_two, i)
 
@@ -386,9 +391,11 @@
         spread = jnp.broadcast_to(table_ref[h : h + 1, :], (seq, 2 * seq))
         bias[h] = pltpu.roll(spread, seq + 1, 1, stride=1, stride_axis=0)[:, :seq]
     loads[0].wait()
-    chosen = selection(local, wide, head_size, False)
     for j in range(3):
-        w_qkv[j] = mm(w_raw[j], chosen).astype(BF)
+        low = j * local // LANES * LANES
+        high = -(-(j + 1) * local // LANES) * LANES
+        chosen = selection(high - low, wide, head_size, False, j * local - low)
+        w_qkv[j] = mm(w_raw[:, low:high], chosen).astype(BF)
     for load in loads[1:]:
         load.wait()
 
@@ -401,48 +408,102 @@
     def share_of(index):
         return pl.ds(pl.multiple_of(index * share, 8), share)
 
-    def slot(array, index, j):
-        return array.at[index] if j is None else array.at[index, j]
-
-    jobs = [
-        (grad_two, active, w_back, back_grad_ref, None),
-        (normed_two, grad_hidden, w_in, in_grad_ref, None),
-        (grad_one, mixed_heads, thin, out_grad_ref, None),
-    ] + [(normed, grad_qkv.at[j], w_raw.at[j], qkv_grad_ref, j) for j in range(3)]
-    tile = width // 3
+    jobs = (
+        (w_back, back_grad_ref),
+        (w_in, in_grad_ref),
+        (w_raw, thin_grad_ref),
+    )
+    paired = shares == 4
+    half = replica // 2
+    partner = replica + 1 - 2 * lax.rem(replica, 2)
+    inner = (replica == 1) | (replica == 2)
+
+    def across(c):
+        return 2 - half if c else 3 * (1 - half)
 
     def own_copy(k):
-        _, _, buf, dst, j = jobs[k]
+        buf, dst = jobs[k]
         return pltpu.make_async_copy(
-            buf.at[share_of(replica)], slot(dst, replica, j), weight_own.at[k]
+            buf.at[share_of(replica)], dst.at[0 if paired else replica], weight_own.at[k]
         )
 
-    def weight_copy(k, d, index):
-        _, _, buf, dst, j = jobs[k]
+    def weight_copy(k, index, dst, send, recv, device):
         return pltpu.make_async_remote_copy(
-            src_ref=buf.at[share_of(replica_peer(d))],
-            dst_ref=slot(dst, index, j),
-            send_sem=weight_send.at[k, d - 1],
-            recv_sem=weight_recv.at[k, d - 1],
-            device_id={"dp": replica_peer(d)},
+            src_ref=jobs[k][0].at[share_of(index)],
+            dst_ref=dst,
+            send_sem=weight_send.at[k, send],
+            recv_sem=weight_recv.at[k, recv],
+            device_id={"dp": device},
         )
 
+    def near_copy(k):
+        return weight_copy(k, partner, jobs[k][1].at[1], 0, 0, partner)
+
+    def cross_copy(k, c):
+        return weight_copy(k, across(c), crossed.at[k, c], 1 + c, 1 + c, partner)
+
+    def forward_copy(k, c):
+        return weight_copy(k, across(c), jobs[k][1].at[2], 1 + c, 3, across(c))
+
+    def direct_copy(k, d, index):
+        to = replica_peer(d)
+        return weight_copy(k, to, jobs[k][1].at[index], d - 1, d - 1, to)
+
     def weight_job(k):
-        left, right, buf, _, _ = jobs[k]
+        tile = LANES if k == 2 else width // 3
 
         def tile_step(t, carry):
             where = pl.ds(pl.multiple_of(t * tile, LANES), tile)
-            buf[where, :] = mm(left[:, where], right[...], 0, 0).astype(BF)
+            if k == 0:
+                out = mm(grad_two[:, where], active[...], 0, 0)
+            elif k == 1:
+                out = mm(normed_two[:, where], grad_hidden[...], 0, 0)
+            else:
+                left = normed[:, where]
+                out = [mm(left, grad_qkv[j], 0, 0) for j in range(3)]
+                out.append(mm(grad_one[:, where], mixed_heads[...], 0, 0))
+                out = jnp.concatenate(out, axis=1)
+            jobs[k][0][where, :] = out.astype(BF)
             return carry
 
-        lax.fori_loop(0, 3, tile_step, 0)
+        lax.fori_loop(0, width // tile, tile_step, 0)
         own_copy(k).start()
-        for d in range(1, shares):
-            weight_copy(k, d, replica).start()
-
-    def qkv_jobs(i):
-        for k in range(3, 6):
-            weight_job(k)
+        if paired:
+
+            @pl.when(jnp.logical_not(inner))
+            def _():
+                cross_copy(k, 0).start()
+                cross_copy(k, 1).start()
+
+            near_copy(k).start()
+        else:
+            for d in range(1, shares):
+                direct_copy(k, d, replica).start()
+
+    def relay(k):
+        if paired:
+
+            @pl.when(inner)
+            def _():
+                buf = jobs[k][0]
+                for c in range(2):
+                    where = share_of(across(c))
+                    cross_copy(k, c).wait_recv()
+                    pair = buf[where, :].astype(F32) + crossed[k, c].astype(F32)
+                    buf[where, :] = pair.astype(BF)
+                    forward_copy(k, c).start()
+
+    def weight_wait(k):
+        own_copy(k).wait()
+        if paired:
+            near_copy(k).wait()
+            for c in range(2):
+                cross_copy(k, c).wait_send()
+            forward_copy(k, 0).wait_recv()
+        else:
+            for d in range(1, shares):
+                direct_copy(k, d, replica).wait_send()
+                direct_copy(k, d, replica_source(d)).wait_recv()
 
     def later_enter(i):
         @pl.when(section == 1)
@@ -450,20 +511,21 @@
             enter(i)
 
     schedule = (
-        (grad_enter, 11, 14, count),
-        (attend, 2, 2, count),
-        (middle, 3, 3, count),
         (later_enter, 0, 0, count),
-        (leave, 6, 10, count),
-        (feed_back, 15, 10, count),
-        (grad_leave, 31, 17, count),
-        (feed, 4, 7, count),
-        (lambda i: weight_job(2), 31, 17, 1),
-        (qkv_jobs, 30, 19, 1),
-        (lambda i: weight_job(1), 17, 18, 1),
-        (middle_back, 23, 12, count),
-        (attend_back, 26, 14, count),
-        (lambda i: weight_job(0), 24, 19, 1),
+        (lambda i: weight_job(0), 14, 16, 1),
+        (feed_back, 11, 8, count),
+        (grad_enter, 8, 21, count),
+        (lambda i: weight_job(1), 18, 10, 1),
+        (attend, 1, 1, count),
+        (grad_leave, 19, 19, count),
+        (middle, 2, 2, count),
+        (lambda i: relay(1), 21, 19, 1),
+        (middle_back, 14, 14, count),
+        (attend_back, 17, 16, count),
+        (feed, 3, 4, count),
+        (lambda i: weight_job(2), 20, 21, 1),
+        (leave, 4, 7, count),
+        (lambda i: relay(0), 18, 21, 1),
     )
     steps = max(max(first, second) for _, first, second, _ in schedule) + count
 
@@ -511,6 +573,7 @@
             for h, c in enumerate(carried)
         ]
 
+    relay(2)
     carried = lax.fori_loop(0, seq // 8, shift_add, carried)
     behind = 7 - lax.broadcasted_iota(jnp.int32, (8, lanes), 0)
     for h in range(heads):
@@ -543,11 +606,8 @@
     for k in range(4):
         for d in range(1, shares):
             tiny_copy(k, d, replica).start()
-    for k in range(6):
-        own_copy(k).wait()
-        for d in range(1, shares):
-            weight_copy(k, d, replica).wait_send()
-            weight_copy(k, d, replica_source(d)).wait_recv()
+    for k in range(3):
+        weight_wait(k)
     for k in range(4):
         for d in range(1, shares):
             tiny_copy(k, d, replica).wait_send()
@@ -561,6 +621,7 @@
     wide = heads * LANES
     share = width // shares
     total = count * seq
+    blocks = 3 if shares == 4 else shares
     vmem = pl.BlockSpec(memory_space=pltpu.VMEM)
     anywhere = pl.BlockSpec(memory_space=pl.ANY)
     dma = pltpu.SemaphoreType.DMA
@@ -572,15 +633,14 @@
             jax.ShapeDtypeStruct((shares, heads, 2 * seq), F32),
             jax.ShapeDtypeStruct((shares, count, 2, wide), F32),
             jax.ShapeDtypeStruct((shares, count, width), BF),
-            jax.ShapeDtypeStruct((shares, 3, share, local_width), BF),
-            jax.ShapeDtypeStruct((shares, share, local_width), BF),
-            jax.ShapeDtypeStruct((shares, share, hidden_width), BF),
-            jax.ShapeDtypeStruct((shares, share, hidden_width), BF),
+            jax.ShapeDtypeStruct((blocks, share, 4 * local_width), BF),
+            jax.ShapeDtypeStruct((blocks, share, hidden_width), BF),
+            jax.ShapeDtypeStruct((blocks, share, hidden_width), BF),
         ),
         in_specs=[
             pl.BlockSpec(memory_space=pltpu.SMEM),
             anywhere,
-            vmem,
+            anywhere,
             vmem,
             vmem,
             anywhere,
@@ -593,9 +653,9 @@
             vmem,
             vmem,
         ],
-        out_specs=(vmem, vmem, vmem, vmem, vmem, anywhere, anywhere, anywhere, anywhere),
+        out_specs=(vmem, vmem, vmem, vmem, vmem, anywhere, anywhere, anywhere),
         scratch_shapes=[
-            pltpu.VMEM((3, width, local_width), BF),
+            pltpu.VMEM((width, 4 * local_width), BF),
             pltpu.VMEM((3, width, wide), BF),
             pltpu.VMEM((local_width, width), BF),
             pltpu.VMEM((width, hidden_width), BF),
@@ -618,7 +678,7 @@
             pltpu.VMEM((count, rows, width), BF),
             pltpu.VMEM((count, rows, width), BF),
             pltpu.VMEM((count, rows, width), F32),
-            pltpu.VMEM((width, local_width), BF),
+            pltpu.VMEM((3, 2, share, hidden_width), BF),
             pltpu.VMEM((8, width), F32),
             pltpu.VMEM((n, 8, width), F32),
             dma((5,)),
@@ -628,9 +688,9 @@
             dma((4, count, n - 1)),
             dma((2, count)),
             dma((2, count)),
-            dma((6, shares - 1)),
-            dma((6, shares - 1)),
-            dma((6,)),
+            dma((3, shares)),
+            dma((3, shares)),
+            dma((3,)),
             dma((4, shares - 1)),
             dma((4, shares - 1)),
             dma((n - 1,)),
@@ -685,7 +745,7 @@
             cotangent,
             time_part,
             norms[0],
-            jnp.transpose(qkv_weight[0], (1, 0, 2)),
+            jnp.pad(qkv_weight[0].reshape(width, 3 * local_width), ((0, 0), (0, local_width))),
             out_weight[0],
             out_bias,
             mlp_in_weight[0],
@@ -696,7 +756,7 @@
             time_rows,
         ),
     )
-    boundary, small, table_grad, columns, all_rows, qkv_grad, out_grad, in_grad, back_grad = outs
+    boundary, small, table_grad, columns, all_rows, thin_grad, in_grad, back_grad = outs
     columns = columns.reshape(shares * count, 2, heads, LANES)[..., :head_size]
     columns = columns.reshape(shares * count, 2 * local_width)
     all_rows = lax.dynamic_slice_in_dim(
@@ -714,13 +774,14 @@
         return jnp.sum(value.astype(F32), axis=0)
 
     small = added(small)
+    thin_grad = added(thin_grad)
     table_grad = jnp.flip(added(table_grad)[:, : rel_bias.shape[2]], axis=1)
     return (
         boundary[None],
         small[None, :4],
-        jnp.transpose(added(qkv_grad), (1, 0, 2))[None],
+        thin_grad[:, : 3 * local_width].reshape(share, 3, local_width)[None],
         time_grad[None],
-        added(out_grad).T[None],
+        thin_grad[:, 3 * local_width :].T[None],
         small[4][None],
         added(in_grad)[None],
         small[6][None],

time: 380 us -> 300 us (0.79)
  Pallas kernels: 348 us -> 266 us
  local copies, waits for them, and re-layouts: 14.9 us -> 19.8 us
    pallas_call x1, Pallas kernels: 348 us -> 266 us  [run_layer(): pl.pallas_call(functools.partial(layer_kernel, sizes), out_shape=(jax.Sha...]
    unnamed x26 -> x24, local copies, waits for them, and re-layouts: 9.37 us -> 6.74 us
where the time goes in v4:
time: 300 us
  Pallas kernels  266 us (89%)
  local copies, waits for them, and re-layouts  19.8 us (7%)
  between operations  6.61 us (2%)
  other arithmetic  4.84 us (2%)
    pallas_call x1, Pallas kernels, run_layer(): pl.pallas_call(functools.partial(layer_kernel, sizes), out_shape=(jax.Sha...  266 us
    unnamed x24, local copies, waits for them, and re-layouts  6.74 us

profile of v4, /device:TPU:0, one launch (start us, length us, event | category | flops | bytes accessed | tf_op | source)
XLA Modules:
  0.0 300.0 jit_solution(11760051541025858948)
XLA Ops:
  0.6 1.4 fusion.7
  7.8 0.8 constant_dynamic-slice_fusion.2
  8.6 0.0 copy-start.3
  8.6 0.6 copy-done.3
  9.2 1.9 fusion.3
  11.2 0.6 reshape.41.time_ref
  11.8 2.9 copy.35
  14.7 0.0 copy-start.7
  14.7 1.7 pad.13.qkv_raw_ref
  16.5 0.0 copy-done.7
  16.5 0.4 reverse
  16.9 0.1 slice.54
  17.0 0.6 pad.14.table_ref
  17.6 266.2 %two_pass.1 = (f32[3,80,1152]{2,1,0:T(8,128)}, f32[4,8,1152]{2,1,0:T(8,128)}, f32[4,4,640]{2,1,0:T(4,128)}, f32[4,3,2,512]{3,2,1,0:T(2,128)}, bf16[4,3,1152]{2,1...) custom-call(s32[3]{0:T(128)} %lengths_ref.1, ...), custom_call_target="tpu_custom_call" | custom-call | tf_op jit(solution)/shard_map/two_pass/pallas_call | solution.py:628
  283.8 0.0 copy-start.4
  283.8 0.0 copy-start.6
  283.8 4.5 %convert_reduce_fusion = (f32[288,1152]{1,0:T(8,128)}, f32[288,1152]{1,0:T(8,128)}) fusion(bf16[3,288,1152]{2,1,0:T(8,128)(2,1)} %get-tuple-element.25, bf16[3,288,1152]{2,1,0:T(8,128)(2,1)} %get-tuple-element.24), kind=kLoop, calls=%fused_computation | loop fusion | flops 3317760 | bytes 6635520 | tf_op jit(solution)/shard_map/reduce_sum | solution.py:774
  288.3 0.0 copy-start
  288.3 0.0 copy-done.4
  288.4 0.1 reshape.44
  288.5 0.1 dot_general.20
  288.6 0.0 copy-done.6
  288.6 0.6 convolution_bitcast_fusion
  289.3 1.6 copy.39
  290.9 0.0 copy-done
  290.9 0.3 convert_reduce_fusion.2
  291.2 1.0 slice.45
  292.2 1.6 copy.36
  293.9 0.0 copy-start.2
  293.9 0.0 copy-start.5
  293.9 1.6 copy.38
  295.4 0.0 copy-start.1
  295.5 0.2 slice_bitcast_fusion
  295.6 1.0 copy.40
  296.6 0.0 copy-done.2
  296.6 0.6 slice_bitcast_fusion.1
  297.2 0.6 fusion.6
  297.8 0.0 copy-done.5
  297.9 0.5 reverse.1
  298.3 0.7 slice_bitcast_fusion.2
  299.0 0.0 copy-done.1
  299.0 1.0 copy.46
  (7 shorter events, 0.2 us)
Async XLA Ops:
  8.6 0.6 copy-start.3
  14.7 1.8 copy-start.7
  283.8 4.5 %copy-start.4 = (f32[4,3,2,512]{3,2,1,0:T(2,128)S(1)}, f32[4,3,2,512]{3,2,1,0:T(2,128)}, u32[]{:S(2)}) copy-start(f32[4,3,2,512]{3,2,1,0:T(2,128)} %get-tuple-element.23) | copy-start | bytes 147460
  283.8 4.8 %copy-start.6 = (bf16[4,3,1152]{2,1,0:T(4,128)(2,1)S(1)}, bf16[4,3,1152]{2,1,0:T(4,128)(2,1)}, u32[]{:S(2)}) copy-start(bf16[4,3,1152]{2,1,0:T(4,128)(2,1)} %get-tuple-element.22) | copy-start | bytes 82948
  288.3 2.5 copy-start
  293.9 2.8 copy-start.2
  293.9 4.0 %copy-start.5 = (f32[4,4,640]{2,1,0:T(4,128)S(1)}, f32[4,4,640]{2,1,0:T(4,128)}, u32[]{:S(2)}) copy-start(f32[4,4,640]{2,1,0:T(4,128)} %get-tuple-element.26) | copy-start | bytes 122884
  295.4 3.6 %copy-start.1 = (f32[3,80,1152]{2,1,0:T(8,128)S(1)}, f32[3,80,1152]{2,1,0:T(8,128)}, u32[]{:S(2)}) copy-start(f32[3,80,1152]{2,1,0:T(8,128)} %get-tuple-element.19) | copy-start | bytes 3317764

commit v5 on v4

--- a/solution.py
+++ b/solution.py
@@ -23,12 +23,12 @@
     )
 
 
-def selection(rows, cols, head_size, flip, first=0):
+def selection(rows, cols, head_size, flip):
     shape = (cols, rows) if flip else (rows, cols)
     row = lax.broadcasted_iota(jnp.int32, shape, 1 if flip else 0)
     col = lax.broadcasted_iota(jnp.int32, shape, 0 if flip else 1)
     within = col & (LANES - 1)
-    hit = (within < head_size) & (row - first == (col // LANES) * head_size + within)
+    hit = (within < head_size) & (row == (col // LANES) * head_size + within)
     return jnp.where(hit, 1.0, 0.0).astype(BF)
 
 
@@ -145,7 +145,7 @@
     loads = [
         pltpu.make_async_copy(a, b, load_sem.at[k])
         for k, (a, b) in enumerate(
-            [(qkv_raw_ref, w_raw), (out_w_ref, w_out), (in_w_ref, w_in), (back_w_ref, w_back)]
+            [(qkv_raw_ref, w_raw.at[0 : 3 * local]), (out_w_ref, w_out), (in_w_ref, w_in), (back_w_ref, w_back)]
         )
     ]
     for load in loads:
@@ -223,7 +223,7 @@
         gather_wait(0, normed, i)
         here = image_of(i)
         for j in range(3):
-            linear = mm(normed[here, :], w_qkv[j])
+            linear = mm(normed[here, :], w_qkv[j], 1, 1)
             if j == 0:
                 linear = linear + time_ref[i, 0:1, :]
             if j == 2:
@@ -331,7 +331,7 @@
         chosen = selection(local, wide, head_size, True)
         for j in range(3):
             grad = jnp.concatenate(outs[j], axis=1)
-            term = mm(grad, w_qkv[j], 1, 1)
+            term = mm(grad, w_qkv[j])
             total = term if total is None else total + term
             grad_qkv[j, here, :] = mm(grad, chosen).astype(BF)
             if j != 1:
@@ -391,11 +391,9 @@
         spread = jnp.broadcast_to(table_ref[h : h + 1, :], (seq, 2 * seq))
         bias[h] = pltpu.roll(spread, seq + 1, 1, stride=1, stride_axis=0)[:, :seq]
     loads[0].wait()
+    chosen = selection(local, wide, head_size, True)
     for j in range(3):
-        low = j * local // LANES * LANES
-        high = -(-(j + 1) * local // LANES) * LANES
-        chosen = selection(high - low, wide, head_size, False, j * local - low)
-        w_qkv[j] = mm(w_raw[:, low:high], chosen).astype(BF)
+        w_qkv[j] = mm(chosen, w_raw[j * local : (j + 1) * local, :]).astype(BF)
     for load in loads[1:]:
         load.wait()
 
@@ -413,6 +411,7 @@
         (w_in, in_grad_ref),
         (w_raw, thin_grad_ref),
     )
+    tile = width // 3
     paired = shares == 4
     half = replica // 2
     partner = replica + 1 - 2 * lax.rem(replica, 2)
@@ -450,10 +449,9 @@
         return weight_copy(k, to, jobs[k][1].at[index], d - 1, d - 1, to)
 
     def weight_job(k):
-        tile = LANES if k == 2 else width // 3
-
         def tile_step(t, carry):
-            where = pl.ds(pl.multiple_of(t * tile, LANES), tile)
+            place = 2 - t + half * (2 * t - 2) if paired else t
+            where = pl.ds(pl.multiple_of(place * tile, LANES), tile)
             if k == 0:
                 out = mm(grad_two[:, where], active[...], 0, 0)
             elif k == 1:
@@ -464,17 +462,18 @@
                 out.append(mm(grad_one[:, where], mixed_heads[...], 0, 0))
                 out = jnp.concatenate(out, axis=1)
             jobs[k][0][where, :] = out.astype(BF)
+            if paired:
+                for c in range(2):
+
+                    @pl.when(jnp.logical_not(inner) & (t == c))
+                    def _(c=c):
+                        cross_copy(k, c).start()
+
             return carry
 
-        lax.fori_loop(0, width // tile, tile_step, 0)
+        lax.fori_loop(0, 3, tile_step, 0)
         own_copy(k).start()
         if paired:
-
-            @pl.when(jnp.logical_not(inner))
-            def _():
-                cross_copy(k, 0).start()
-                cross_copy(k, 1).start()
-
             near_copy(k).start()
         else:
             for d in range(1, shares):
@@ -656,7 +655,7 @@
         out_specs=(vmem, vmem, vmem, vmem, vmem, anywhere, anywhere, anywhere),
         scratch_shapes=[
             pltpu.VMEM((width, 4 * local_width), BF),
-            pltpu.VMEM((3, width, wide), BF),
+            pltpu.VMEM((3, wide, width), BF),
             pltpu.VMEM((local_width, width), BF),
             pltpu.VMEM((width, hidden_width), BF),
             pltpu.VMEM((hidden_width, width), BF),
@@ -728,9 +727,8 @@
     shares = lax.axis_size("dp")
     share = width // shares
     sizes = (lax.axis_size("mp"), count, rows, width, hidden_width, heads, head_size, shares)
-    time_rows = jnp.concatenate(
-        [lax.dynamic_slice_in_dim(time_table, timesteps[i], 1, axis=0) for i in range(count)]
-    )
+    chosen = jax.nn.one_hot(timesteps, time_table.shape[0], dtype=BF)
+    time_rows = jnp.dot(chosen, time_table, preferred_element_type=F32).astype(BF)
     time_part = jnp.dot(
         time_rows, time_weight[0].reshape(width, 2 * local_width), preferred_element_type=F32
     ).reshape(count, 2, heads, head_size)
@@ -745,7 +743,7 @@
             cotangent,
             time_part,
             norms[0],
-            jnp.pad(qkv_weight[0].reshape(width, 3 * local_width), ((0, 0), (0, local_width))),
+            jnp.transpose(qkv_weight[0], (1, 2, 0)).reshape(3 * local_width, width),
             out_weight[0],
             out_bias,
             mlp_in_weight[0],

time: 300 us -> 286 us (0.953)
  local copies, waits for them, and re-layouts: 19.8 us -> 12 us
  between operations: 6.61 us -> 0.75 us
  Pallas kernels: 266 us -> 263 us
    unnamed x24 -> x20, local copies, waits for them, and re-layouts: 6.74 us -> 6.3 us
where the time goes in v5:
time: 286 us
  Pallas kernels  263 us (92%)
  local copies, waits for them, and re-layouts  12 us (4%)
  other arithmetic  6.14 us (2%)
  matrix products  3.47 us (1%)
    pallas_call x1, Pallas kernels, run_layer(): pl.pallas_call(functools.partial(layer_kernel, sizes), out_shape=(jax.Sha...  263 us
    unnamed x20, local copies, waits for them, and re-layouts  6.3 us
    reduce_sum x4, other arithmetic, added(): return jnp.sum(value.astype(F32), axis=0)  6.14 us

profile of v5, /device:TPU:0, one launch (start us, length us, event | category | flops | bytes accessed | tf_op | source)
XLA Modules:
  0.0 285.8 jit_solution(7568556667509882428)
XLA Ops:
  0.6 0.0 copy-start.5
  0.7 0.0 copy-start.2
  0.7 2.2 convolution_convert_fusion.steps_ref
  2.9 0.0 copy-done.5
  2.9 0.0 copy-start.4
  2.9 0.5 reverse
  3.4 0.1 slice.42
  3.4 0.6 pad.9.table_ref
  4.1 0.0 copy-done.2
  4.1 0.6 fusion.3
  4.7 0.0 copy-done.4
  4.7 0.6 reshape.45.time_ref
  5.3 263.5 %two_pass.1 = (f32[3,80,1152]{2,1,0:T(8,128)}, f32[4,8,1152]{2,1,0:T(8,128)}, f32[4,4,640]{2,1,0:T(4,128)}, f32[4,3,2,512]{3,2,1,0:T(2,128)}, bf16[4,3,1152]{2,1...) custom-call(s32[3]{0:T(128)} %lengths_ref.1, ...), custom_call_target="tpu_custom_call" | custom-call | tf_op jit(solution)/shard_map/two_pass/pallas_call | solution.py:627
  268.8 0.0 copy-start.1
  268.8 0.9 reduce_sum.49
  269.8 0.9 reduce_sum.45
  270.7 0.5 reverse.1
  271.2 0.7 slice_bitcast_fusion.2
  271.9 0.6 fusion.7
  272.5 0.6 slice_bitcast_fusion.1
  273.1 0.8 reshape.47
  273.9 0.8 reshape.48
  274.7 0.1 reshape.49
  274.8 0.1 dot_general.24
  274.9 0.6 convolution_bitcast_fusion
  275.6 1.6 copy.36
  277.2 0.0 copy-done.1
  277.2 0.3 convert_reduce_fusion.2
  277.5 0.2 slice_bitcast_fusion
  277.6 0.1 slice.33
  277.7 1.0 copy.37
  278.7 0.4 copy.33
  279.1 0.0 copy-start
  279.1 1.6 copy.35
  280.7 0.1 copy-done
  280.8 0.0 copy-start.3
  280.8 4.0 %convert_reduce_fusion = (f32[288,1152]{1,0:T(8,128)}, f32[288,1152]{1,0:T(8,128)}) fusion(bf16[3,288,1152]{2,1,0:T(8,128)(2,1)} %get-tuple-element.25, bf16[3,288,1152]{2,1,0:T(8,128)(2,1)S(1)} %copy-done), kind=kLoop, calls=%fused_computation | loop fusion | flops 3317760 | bytes 6635520 | tf_op jit(solution)/shard_map/reduce_sum | solution.py:772
  284.8 0.0 copy-done.3
  284.8 1.0 copy.43
  (2 shorter events, 0.0 us)
Async XLA Ops:
  0.6 2.2 copy-start.5
  0.7 3.4 %copy-start.2 = (bf16[1,1152,2,288]{1,3,2,0:T(8,128)(2,1)S(1)}, bf16[1,1152,2,288]{1,3,2,0:T(8,128)(2,1)}, u32[]{:S(2)}) copy-start(bf16[1,1152,2,288]{1,3,2,0:T(8,128)(2,1)} %param.22) | copy-start | bytes 3981316
  2.9 1.8 copy-start.4
  268.8 8.3 %copy-start.1 = (bf16[3,288,1152]{2,1,0:T(8,128)(2,1)S(1)}, bf16[3,288,1152]{2,1,0:T(8,128)(2,1)}, u32[]{:S(2)}) copy-start(bf16[3,288,1152]{2,1,0:T(8,128)(2,1)} %get-tuple-element.21) | copy-start | bytes 5971972
  279.1 1.7 copy-start
  280.8 4.0 %copy-start.3 = (f32[3,80,1152]{2,1,0:T(8,128)S(1)}, f32[3,80,1152]{2,1,0:T(8,128)}, u32[]{:S(2)}) copy-start(f32[3,80,1152]{2,1,0:T(8,128)} %get-tuple-element.19) | copy-start | bytes 3317764

commit v6 on v5

--- a/solution.py
+++ b/solution.py
@@ -278,7 +278,7 @@
 
         @pl.when(section == 1)
         def _():
-            boundary_ref[i] = jnp.where(row_mask(i), out, 0.0)
+            boundary_ref[0, i] = jnp.where(row_mask(i), out, 0.0)
 
     def grad_enter(i):
         @pl.when(section == 0)
@@ -287,7 +287,10 @@
             gather_start(2, grad_two, i)
 
     def feed_back(i):
-        gather_wait(2, grad_two, i)
+        @pl.when(section == 0)
+        def _():
+            gather_wait(2, grad_two, i)
+
         here = image_of(i)
         grad_active = mm(grad_two[here, :], w_back[...], 1, 1)
         held = (slope[here, :] * grad_active).astype(BF)
@@ -353,7 +356,7 @@
 
         @pl.when(section == 0)
         def _():
-            boundary_ref[i] = total
+            boundary_ref[0, i] = total
 
         sums[0:1, :] += gain
         sums[1:2, :] += offset
@@ -397,6 +400,10 @@
     for load in loads[1:]:
         load.wait()
 
+    @pl.when(section == 1)
+    def _():
+        each(lambda i: gather_wait(2, grad_two, i))
+
     def replica_peer(d):
         return lax.rem(replica + d, shares)
 
@@ -407,9 +414,9 @@
         return pl.ds(pl.multiple_of(index * share, 8), share)
 
     jobs = (
-        (w_back, back_grad_ref),
-        (w_in, in_grad_ref),
-        (w_raw, thin_grad_ref),
+        (w_raw, back_grad_ref),
+        (w_back, in_grad_ref),
+        (w_in, thin_grad_ref),
     )
     tile = width // 3
     paired = shares == 4
@@ -448,36 +455,41 @@
         to = replica_peer(d)
         return weight_copy(k, to, jobs[k][1].at[index], d - 1, d - 1, to)
 
+    def weight_step(k, t):
+        place = 2 - t + half * (2 * t - 2) if paired else t
+        where = pl.ds(pl.multiple_of(place * tile, LANES), tile)
+        if k == 0:
+            out = mm(grad_two[:, where], active[...], 0, 0)
+        elif k == 1:
+            out = mm(normed_two[:, where], grad_hidden[...], 0, 0)
+        else:
+            left = normed[:, where]
+            out = [mm(left, grad_qkv[j], 0, 0) for j in range(3)]
+            out.append(mm(grad_one[:, where], mixed_heads[...], 0, 0))
+            out = jnp.concatenate(out, axis=1)
+        jobs[k][0][where, :] = out.astype(BF)
+        if paired:
+            for c in range(2):
+
+                @pl.when(jnp.logical_not(inner) & (t == c))
+                def _(c=c):
+                    cross_copy(k, c).start()
+
+        @pl.when(t == 2)
+        def _():
+            own_copy(k).start()
+            if paired:
+                near_copy(k).start()
+            else:
+                for d in range(1, shares):
+                    direct_copy(k, d, replica).start()
+
     def weight_job(k):
-        def tile_step(t, carry):
-            place = 2 - t + half * (2 * t - 2) if paired else t
-            where = pl.ds(pl.multiple_of(place * tile, LANES), tile)
-            if k == 0:
-                out = mm(grad_two[:, where], active[...], 0, 0)
-            elif k == 1:
-                out = mm(normed_two[:, where], grad_hidden[...], 0, 0)
-            else:
-                left = normed[:, where]
-                out = [mm(left, grad_qkv[j], 0, 0) for j in range(3)]
-                out.append(mm(grad_one[:, where], mixed_heads[...], 0, 0))
-                out = jnp.concatenate(out, axis=1)
-            jobs[k][0][where, :] = out.astype(BF)
-            if paired:
-                for c in range(2):
-
-                    @pl.when(jnp.logical_not(inner) & (t == c))
-                    def _(c=c):
-                        cross_copy(k, c).start()
-
+        def step(t, carry):
+            weight_step(k, t)
             return carry
 
-        lax.fori_loop(0, 3, tile_step, 0)
-        own_copy(k).start()
-        if paired:
-            near_copy(k).start()
-        else:
-            for d in range(1, shares):
-                direct_copy(k, d, replica).start()
+        lax.fori_loop(0, 3, step, 0)
 
     def relay(k):
         if paired:
@@ -511,20 +523,20 @@
 
     schedule = (
         (later_enter, 0, 0, count),
-        (lambda i: weight_job(0), 14, 16, 1),
+        (lambda i: weight_step(0, i), 14, 7, 3),
         (feed_back, 11, 8, count),
         (grad_enter, 8, 21, count),
-        (lambda i: weight_job(1), 18, 10, 1),
+        (lambda i: weight_step(1, i), 17, 10, 3),
         (attend, 1, 1, count),
         (grad_leave, 19, 19, count),
         (middle, 2, 2, count),
-        (lambda i: relay(1), 21, 19, 1),
+        (lambda i: relay(1), 22, 19, 1),
         (middle_back, 14, 14, count),
         (attend_back, 17, 16, count),
         (feed, 3, 4, count),
-        (lambda i: weight_job(2), 20, 21, 1),
+        (lambda i: weight_job(2), 19, 21, 1),
         (leave, 4, 7, count),
-        (lambda i: relay(0), 18, 21, 1),
+        (lambda i: relay(0), 18, 15, 1),
     )
     steps = max(max(first, second) for _, first, second, _ in schedule) + count
 
@@ -627,7 +639,7 @@
     return pl.pallas_call(
         functools.partial(layer_kernel, sizes),
         out_shape=(
-            jax.ShapeDtypeStruct((count, rows, width), F32),
+            jax.ShapeDtypeStruct((1, count, rows, width), F32),
             jax.ShapeDtypeStruct((shares, 8, width), F32),
             jax.ShapeDtypeStruct((shares, heads, 2 * seq), F32),
             jax.ShapeDtypeStruct((shares, count, 2, wide), F32),
@@ -769,17 +781,19 @@
     ).reshape(share, 2, local_width)
 
     def added(value):
-        return jnp.sum(value.astype(F32), axis=0)
+        return functools.reduce(jnp.add, [value[k].astype(F32) for k in range(value.shape[0])])
 
     small = added(small)
-    thin_grad = added(thin_grad)
+    thin_parts = [
+        added(thin_grad[:, :, j * local_width : (j + 1) * local_width]) for j in range(4)
+    ]
     table_grad = jnp.flip(added(table_grad)[:, : rel_bias.shape[2]], axis=1)
     return (
-        boundary[None],
+        boundary,
         small[None, :4],
-        thin_grad[:, : 3 * local_width].reshape(share, 3, local_width)[None],
+        jnp.transpose(jnp.stack(thin_parts[:3]), (1, 0, 2))[None],
         time_grad[None],
-        thin_grad[:, 3 * local_width :].T[None],
+        thin_parts[3].T[None],
         small[4][None],
         added(in_grad)[None],
         small[6][None],

time: 286 us -> 280 us (0.979)
  Pallas kernels: 263 us -> 258 us
    reduce_sum x4 -> x0, other arithmetic: 6.14 us -> none  [added(): return jnp.sum(value.astype(F32), axis=0)]
    broadcast_in_dim x0 -> x3, other arithmetic: none -> 5.92 us  [the longest x1 2.3 us: local(): jnp.transpose(jnp.stack(thin_parts[:3]), (1, 0, 2))[None]]
    pallas_call x1, Pallas kernels: 263 us -> 258 us  [run_layer(): pl.pallas_call(functools.partial(layer_kernel, sizes), out_shape=(jax.Sha...]
    unnamed x20 -> x21, local copies, waits for them, and re-layouts: 6.3 us -> 4.58 us
where the time goes in v6:
time: 280 us; the launch traced here: 279 us
  Pallas kernels  258 us (92%)
  local copies, waits for them, and re-layouts  9.57 us (3%)
  other arithmetic  7.51 us (3%)
  matrix products  3.47 us (1%)
    pallas_call x1, Pallas kernels, run_layer(): pl.pallas_call(functools.partial(layer_kernel, sizes), out_shape=(jax.Sha...  258 us

profile of v6, /device:TPU:0, one launch (start us, length us, event | category | flops | bytes accessed | tf_op | source)
XLA Modules:
  0.0 279.4 jit_solution(407087254176647427)
XLA Ops:
  0.6 0.0 copy-start.6
  0.7 0.0 copy-start.3
  0.7 2.2 convolution_convert_fusion.steps_ref
  2.9 0.0 copy-done.6
  2.9 0.0 copy-start.5
  2.9 0.5 reverse
  3.4 0.1 slice.192
  3.4 0.6 pad.9.table_ref
  4.1 0.0 copy-done.3
  4.1 0.6 fusion.3
  4.7 0.0 copy-done.5
  4.7 0.6 reshape.66.time_ref
  5.3 258.1 %two_pass.1 = (f32[1,3,80,1152]{3,2,1,0:T(8,128)}, f32[4,8,1152]{2,1,0:T(8,128)}, f32[4,4,640]{2,1,0:T(4,128)}, f32[4,3,2,512]{3,2,1,0:T(2,128)}, bf16[4,3,1152]...) custom-call(s32[3]{0:T(128)} %lengths_ref.1, ...), custom_call_target="tpu_custom_call" | custom-call | tf_op jit(solution)/shard_map/two_pass/pallas_call | solution.py:639
  263.4 0.8 add_bitcast_fusion.2
  264.2 0.5 reverse.1
  264.6 0.7 slice_bitcast_fusion.3
  265.3 0.8 slice_add_fusion
  266.1 0.6 slice_bitcast_fusion
  266.7 0.6 slice.157
  267.4 0.8 reshape.68
  268.2 0.8 reshape.69
  269.0 0.1 reshape.70
  269.1 0.1 dot_general.24
  269.2 0.0 copy-start
  269.2 0.6 convolution_bitcast_fusion
  269.9 1.6 copy.31
  271.5 0.0 copy-done
  271.5 0.0 copy-start.2
  271.5 1.7 add_bitcast_fusion.1
  273.1 1.0 copy.32
  274.1 0.0 copy-start.1
  274.1 2.3 maximum_bitcast_fusion
  276.4 0.0 copy-done.2
  276.4 0.0 copy-done.1
  276.4 0.0 copy-start.4
  276.4 1.9 add_bitcast_fusion
  278.4 0.0 copy-done.4
  278.4 1.0 copy.38
  (2 shorter events, 0.0 us)
Async XLA Ops:
  0.6 2.2 copy-start.6
  0.7 3.4 %copy-start.3 = (bf16[1,1152,2,288]{1,3,2,0:T(8,128)(2,1)S(1)}, bf16[1,1152,2,288]{1,3,2,0:T(8,128)(2,1)}, u32[]{:S(2)}) copy-start(bf16[1,1152,2,288]{1,3,2,0:T(8,128)(2,1)} %param.22) | copy-start | bytes 3981316
  2.9 1.8 copy-start.5
  269.2 2.3 copy-start
  271.5 5.0 %copy-start.2 = (bf16[3,288,1152]{2,1,0:T(8,128)(2,1)S(1)}, bf16[3,288,1152]{2,1,0:T(8,128)(2,1)}, u32[]{:S(2)}) copy-start(bf16[3,288,1152]{2,1,0:T(8,128)(2,1)} %get-tuple-element.25) | copy-start | bytes 5971972
  274.1 2.3 copy-start.1
  276.4 1.9 copy-start.4

commit v7 on v6

--- a/solution.py
+++ b/solution.py
@@ -484,13 +484,6 @@
                 for d in range(1, shares):
                     direct_copy(k, d, replica).start()
 
-    def weight_job(k):
-        def step(t, carry):
-            weight_step(k, t)
-            return carry
-
-        lax.fori_loop(0, 3, step, 0)
-
     def relay(k):
         if paired:
 
@@ -534,7 +527,7 @@
         (middle_back, 14, 14, count),
         (attend_back, 17, 16, count),
         (feed, 3, 4, count),
-        (lambda i: weight_job(2), 19, 21, 1),
+        (lambda i: weight_step(2, i), 19, 19, 3),
         (leave, 4, 7, count),
         (lambda i: relay(0), 18, 15, 1),
     )

time: 280 us -> 273 us (0.975)
  Pallas kernels: 258 us -> 252 us
    pallas_call x1, Pallas kernels: 258 us -> 252 us  [run_layer(): pl.pallas_call(functools.partial(layer_kernel, sizes), out_shape=(jax.Sha...]
where the time goes in v7:
time: 273 us
  Pallas kernels  252 us (92%)
  local copies, waits for them, and re-layouts  9.57 us (4%)
  other arithmetic  7.51 us (3%)
  matrix products  3.47 us (1%)
    pallas_call x1, Pallas kernels, run_layer(): pl.pallas_call(functools.partial(layer_kernel, sizes), out_shape=(jax.Sha...  252 us

profile of v7, /device:TPU:0, one launch (start us, length us, event | category | flops | bytes accessed | tf_op | source)
XLA Modules:
  0.0 273.0 jit_solution(15710643055429606424)
XLA Ops:
  0.6 0.0 copy-start.6
  0.7 0.0 copy-start.3
  0.7 2.2 convolution_convert_fusion.steps_ref
  2.9 0.0 copy-done.6
  2.9 0.0 copy-start.5
  2.9 0.5 reverse
  3.4 0.1 slice.192
  3.4 0.6 pad.9.table_ref
  4.1 0.0 copy-done.3
  4.1 0.6 fusion.3
  4.7 0.0 copy-done.5
  4.7 0.6 reshape.66.time_ref
  5.3 251.7 %two_pass.1 = (f32[1,3,80,1152]{3,2,1,0:T(8,128)}, f32[4,8,1152]{2,1,0:T(8,128)}, f32[4,4,640]{2,1,0:T(4,128)}, f32[4,3,2,512]{3,2,1,0:T(2,128)}, bf16[4,3,1152]...) custom-call(s32[3]{0:T(128)} %lengths_ref.1, ...), custom_call_target="tpu_custom_call" | custom-call | tf_op jit(solution)/shard_map/two_pass/pallas_call | solution.py:632
  257.1 0.8 add_bitcast_fusion.2
  257.8 0.5 reverse.1
  258.3 0.7 slice_bitcast_fusion.3
  259.0 0.8 slice_add_fusion
  259.8 0.6 slice_bitcast_fusion
  260.4 0.6 slice.157
  261.0 0.8 reshape.68
  261.8 0.8 reshape.69
  262.7 0.1 reshape.70
  262.8 0.1 dot_general.24
  262.9 0.0 copy-start
  262.9 0.6 convolution_bitcast_fusion
  263.5 1.6 copy.31
  265.1 0.0 copy-done
  265.1 0.0 copy-start.2
  265.1 1.7 add_bitcast_fusion.1
  266.8 1.0 copy.32
  267.8 0.0 copy-start.1
  267.8 2.3 maximum_bitcast_fusion
  270.1 0.0 copy-done.2
  270.1 0.0 copy-done.1
  270.1 0.0 copy-start.4
  270.1 1.9 add_bitcast_fusion
  272.0 0.0 copy-done.4
  272.0 1.0 copy.38
  (2 shorter events, 0.0 us)
Async XLA Ops:
  0.6 2.2 copy-start.6
  0.7 3.4 %copy-start.3 = (bf16[1,1152,2,288]{1,3,2,0:T(8,128)(2,1)S(1)}, bf16[1,1152,2,288]{1,3,2,0:T(8,128)(2,1)}, u32[]{:S(2)}) copy-start(bf16[1,1152,2,288]{1,3,2,0:T(8,128)(2,1)} %param.22) | copy-start | bytes 3981316
  2.9 1.8 copy-start.5
  262.9 2.3 copy-start
  265.1 5.0 %copy-start.2 = (bf16[3,288,1152]{2,1,0:T(8,128)(2,1)S(1)}, bf16[3,288,1152]{2,1,0:T(8,128)(2,1)}, u32[]{:S(2)}) copy-start(bf16[3,288,1152]{2,1,0:T(8,128)(2,1)} %get-tuple-element.25) | copy-start | bytes 5971972
  267.8 2.3 copy-start.1
  270.1 1.9 copy-start.4
